TPU v7x, 768 devices: a whole 4x8x12 slice. The times are simulated.
768 devices in a mesh: wave: 192 (over y_hi, z, x, core), lev: 4 (over y_lo).
Axes of the slice: x: 4, y: 8 (y_hi: 2, y_lo: 4; y = y_hi * 4 + y_lo), z: 12, core: 2. Of those that a mesh axis runs over, the one named last changes fastest.
Arguments:
- spin_tendency: bfloat16 [384, 2, 136, 768], P('wave', None, 'lev'), may hold values from -6 to 6
- spreading_source: bfloat16 [384, 2, 136, 768], P('wave', None, 'lev'), may hold values from -6 to 6
- heat_source: bfloat16 [384, 2, 136, 768], P('wave', None, 'lev'), may hold values from -6 to 6
- helmholtz_inverses: bfloat16 [4, 192, 136, 136], P('lev', 'wave'), may hold values from -0.5 to 0.5
- heat_spreading_coupler: bfloat16 [136, 136], replicated, may hold values from -0.5 to 0.5
- smoothing_strengths: float32 [136], replicated, may hold values from 0.5 to 30
- azimuthal_order_list: int32 [384], P('wave'), may hold values from 0 to 767
Outputs:
- vorticity_new: bfloat16 [384, 2, 136, 768], P('wave', None, 'lev')
- divergence_new: bfloat16 [384, 2, 136, 768], P('wave', None, 'lev')
- temperature_new: bfloat16 [384, 2, 136, 768], P('wave', None, 'lev')
All inputs are finite; a program needn't handle non-finite values.
Results may differ from a plain program's by a relative error of at most 0.0075.
Values may be sent and summed in bfloat16 or wider, within the bound.
No kernel may reach another device: no remote copies, remote signals or barrier semaphores. Data moves between devices by JAX's collectives and lax.ppermute only.
A program may use at most 64 MiB of HBM per device.

v0:
```python
import jax
import jax.numpy as jnp
from jax import lax
from jax.sharding import PartitionSpec as P


def sent_together(arrays, axis, split_dim, concat_dim, along):
    ends, at = ([], 0)
    for a in arrays[:-1]:
        at += a.shape[along]
        ends.append(at)
    both = jnp.concatenate(arrays, axis=along)
    return tuple(
        jnp.split(
            lax.all_to_all(both, axis, split_axis=split_dim, concat_axis=concat_dim, tiled=True),
            ends,
            axis=along,
        )
    )


def damping_table(level_gain, wavenumbers, total_n):
    scaled = (wavenumbers * (wavenumbers + 1)).astype(jnp.float32) / jnp.float32(
        (total_n - 1) * total_n
    )
    return 1.0 / (1.0 + level_gain[:, None] * scaled[None, :] ** 2)


def on_device(
    spin_tendency,
    spreading_source,
    heat_source,
    helmholtz_inverses,
    heat_spreading_coupler,
    smoothing_strengths,
    azimuthal_order_list,
):
    lev_count = lax.axis_size("lev")
    lev_index = lax.axis_index("lev")
    row_count, part_count, lev_local, total_n = spreading_source.shape
    block_n = total_n // lev_count
    layer_count = lev_local * lev_count
    flat_rows = row_count * part_count
    empty_placeholder = jnp.zeros((), jnp.bfloat16)
    rhs_div = lax.all_to_all(spreading_source, "lev", split_axis=3, concat_axis=2, tiled=True)
    stacked = rhs_div.reshape(flat_rows, layer_count, block_n)
    gathered = lax.all_gather(helmholtz_inverses, "wave", axis=1, tiled=True)
    solved_full = jnp.einsum(
        "jkp,bpj->bkj", gathered[0], stacked, preferred_element_type=jnp.float32
    )
    answer_fields = solved_full.astype(jnp.bfloat16)
    coupled = jnp.einsum(
        "om,dms->dos", heat_spreading_coupler, answer_fields, preferred_element_type=jnp.float32
    ).astype(jnp.bfloat16)
    solved_rows = answer_fields.reshape(row_count, part_count, layer_count, block_n)
    coupled_rows = coupled.reshape(row_count, part_count, layer_count, block_n)
    spreading_updated, coupled_out = sent_together((solved_rows, coupled_rows), "lev", 2, 3, 0)
    heat_updated = (heat_source.astype(jnp.float32) - coupled_out.astype(jnp.float32)).astype(
        jnp.bfloat16
    )
    level_gain = lax.dynamic_slice_in_dim(smoothing_strengths, lev_index * lev_local, lev_local)
    damping = damping_table(level_gain, jnp.arange(total_n, dtype=jnp.int32), total_n)
    spin_updated = (spin_tendency.astype(jnp.float32) * damping[None, None]).astype(jnp.bfloat16)
    interior_slice = (
        jnp.arange(total_n, dtype=jnp.int32)[None, :] >= azimuthal_order_list[:, None]
    )[:, None, None, :]
    return (
        jnp.where(interior_slice, spin_updated, empty_placeholder),
        jnp.where(interior_slice, spreading_updated, empty_placeholder),
        jnp.where(interior_slice, heat_updated, empty_placeholder),
    )


def solution(mesh):
    return jax.shard_map(
        on_device,
        mesh=mesh,
        in_specs=(
            P("wave", None, "lev", None),
            P("wave", None, "lev", None),
            P("wave", None, "lev", None),
            P("lev", "wave", None, None),
            P(),
            P(),
            P("wave"),
        ),
        out_specs=(
            P("wave", None, "lev", None),
            P("wave", None, "lev", None),
            P("wave", None, "lev", None),
        ),
        check_vma=False,
    )
```

profile of v0, /device:TPU:1, one launch (start us, length us, event | category | flops | bytes accessed | tf_op | source)
XLA Modules:
  0.0 282.4 jit_solution(8108619773526476913)
XLA Ops:
  7.2 0.0 copy-start
  7.2 0.0 copy-start.4
  7.2 0.0 copy-start.3
  7.2 0.0 all-gather.2.cloned.1.call-start
  7.2 0.7 all-gather.2.cloned.1.call-update
  7.9 2.2 copy.46
  10.1 1.5 reshape.82
  11.7 0.0 copy-start.1
  11.7 0.0 copy-start.2
  11.7 11.0 %all_to_all.30 = bf16[4,2,13056]{2,1,0:T(2,128)(2,1)S(1)} all-to-all(bf16[4,2,13056]{2,1,0:T(2,128)(2,1)S(1)} %reshape.82), channel_id=1, replica_groups=mesh['wave'=192,'lev'=4] {'lev'}, dimensions={0} | all-to-all | bytes 417792 | tf_op jit(solution)/shard_map/all_to_all | solution.py:45
  22.7 2.2 reshape.83
  24.9 0.8 copy.47
  25.7 0.3 reshape.75
  26.0 0.3 copy.49
  26.3 213.7 %all-gather.2.cloned.1.call-done = bf16[1,192,136,136]{3,2,0,1:T(8,128)(2,1)} async-done(((bf16[1,1,136,136]{3,2,0,1:T(8,128)(2,1)}), bf16[1,192,136,136]{3,2,0,1:T(8,128)(2,1)}) %all-gather.2.cloned.1.call-update) | async-done | bytes 7102480 | tf_op jit(solution)/shard_map/all_gather | solution.py:47
  240.0 8.3 %fusion.5 = bf16[4,136,192]{1,0,2:T(4,128)(2,1)S(1)} fusion(bf16[4,136,192]{1,0,2:T(4,128)(2,1)S(1)} %copy.49, bf16[1,192,136,136]{3,2,0,1:T(8,128)(2,1)} %all-gather.2.cloned.1.call-done), kind=kOutput, calls=%fused_computation.4 | convolution fusion | flops 28514304 | bytes 7520256 | tf_op jit(solution)/shard_map/jkp,bpj->bkj/dot_general | solution.py:48
  248.4 0.3 copy.50
  248.7 0.0 copy-done
  248.7 0.2 convolution_convert_fusion
  248.9 0.1 pad_maximum_fusion
  249.0 1.2 copy.52
  250.3 7.9 %all-to-all-start.1 = ((bf16[4,2,136,192]{3,1,0,2:T(2,128)(2,1)}), bf16[4,2,136,192]{3,1,0,2:T(2,128)(2,1)S(1)}, u32[]{:S(2)}, u32[]{:S(2)}) async-start(bf16[4,2,136,192]{3,1,0,2:T(2,128)(2,1)} %copy.52), calls=%async_computation.1 | async-start | bytes 1114112 | tf_op jit(solution)/shard_map/all_to_all | solution.py:15
  258.1 0.0 copy-done.4
  258.1 0.1 dynamic_slice.3
  258.2 0.1 iota_compare_fusion
  258.3 0.1 add_divide_fusion
  258.4 14.5 %all-to-all-done.1 = bf16[4,2,136,192]{3,1,0,2:T(2,128)(2,1)S(1)} async-done(((bf16[4,2,136,192]{3,1,0,2:T(2,128)(2,1)}), bf16[4,2,136,192]{3,1,0,2:T(2,128)(2,1)S(1)}, u32[]{:S(2)}, u32[]{:S(2)}) %all-to-all-start.1) | async-done | bytes 417824 | tf_op jit(solution)/shard_map/all_to_all | solution.py:15
  272.9 0.3 copy.68
  273.2 0.2 slice_convert_fusion
  273.4 0.4 reshape.81
  273.8 0.3 reshape.80
  274.1 1.4 broadcast_select_fusion
  (4 shorter events, 0.0 us)
Async XLA Ops:
  7.2 241.5 %copy-start = (bf16[136,136]{1,0:T(8,128)(2,1)S(1)}, bf16[136,136]{1,0:T(8,128)(2,1)}, u32[]{:S(2)}) copy-start(bf16[136,136]{1,0:T(8,128)(2,1)} %param.11) | copy-start | bytes 110980
  7.2 251.0 %copy-start.4 = (f32[136]{0:T(256)S(1)}, f32[136]{0:T(256)}, u32[]{:S(2)}) copy-start(f32[136]{0:T(256)} %param.12) | copy-start | bytes 1636
  7.2 251.0 %copy-start.3 = (s32[2]{0:T(128)S(1)}, s32[2]{0:T(128)}, u32[]{:S(2)}) copy-start(s32[2]{0:T(128)} %param.13) | copy-start | bytes 28
  7.2 232.8 %all-gather.2.cloned.1.call-start = ((), (), s32[]{:S(2)}) async-start(), calls=%async_computation.2 | async-start | bytes 13438976 | tf_op jit(solution)/shard_map/all_gather | solution.py:47
  11.7 262.4 %copy-start.1 = (bf16[2,2,34,768]{3,1,2,0:T(2,128)(2,1)S(1)}, bf16[2,2,34,768]{3,1,2,0:T(2,128)(2,1)}, u32[]{:S(2)}) copy-start(bf16[2,2,34,768]{3,1,2,0:T(2,128)(2,1)} %param.9) | copy-start | bytes 626692
  11.7 262.4 %copy-start.2 = (bf16[2,2,34,768]{3,1,2,0:T(2,128)(2,1)S(1)}, bf16[2,2,34,768]{3,1,2,0:T(2,128)(2,1)}, u32[]{:S(2)}) copy-start(bf16[2,2,34,768]{3,1,2,0:T(2,128)(2,1)} %param.7) | copy-start | bytes 626692
  250.3 22.6 %all-to-all-start.1 = ((bf16[4,2,136,192]{3,1,0,2:T(2,128)(2,1)}), bf16[4,2,136,192]{3,1,0,2:T(2,128)(2,1)S(1)}, u32[]{:S(2)}, u32[]{:S(2)}) async-start(bf16[4,2,136,192]{3,1,0,2:T(2,128)(2,1)} %copy.52), calls=%async_computation.1 | async-start | bytes 1114112 | tf_op jit(solution)/shard_map/all_to_all | solution.py:15
Sparse Core Ops, SparseCore 0:
  13.6 226.3 all-gather.1
where the time goes:
time: 283 us; the launch traced here: 282 us
  waiting for transfers between devices  229 us (81%)
  between operations  14.2 us (5%)
  blocking collectives  11 us (4%)
  local copies, waits for them, and re-layouts  9.9 us (3%)
  matrix products  8.56 us (3%)
  starting transfers between devices  7.93 us (3%)
    all_gather x1, waiting for transfers between devices, on_device(): gathered = lax.all_gather(helmholtz_inverses, 'wave', axis=1, tiled=True)  214 us
    all_to_all x1, waiting for transfers between devices, sent_together(): lax.all_to_all(both, axis, split_axis=split_dim, concat_axis=concat_dim,...  14.5 us
    all_to_all x1, blocking collectives, on_device(): lax.all_to_all(spreading_source, 'lev', split_axis=3, concat_axis=2, tile...  11 us
    dot_general x1, matrix products, on_device(): jnp.einsum('jkp,bpj->bkj', gathered[0], stacked, preferred_element_type=j...  8.34 us
    all_to_all x1, starting transfers between devices, sent_together(): lax.all_to_all(both, axis, split_axis=split_dim, concat_axis=concat_dim,...  7.89 us
    unnamed x13, local copies, waits for them, and re-layouts  5.93 us
  transfers between devices with their start and end apart: 2, of which 2 were waited for; matrix products, arithmetic and copies ran while one was open for 3% of the time, Pallas kernels for 0%

commit v1 on v0

v1 whole, which is shorter than its diff:
```python
import jax
import jax.numpy as jnp
from jax import lax
from jax.sharding import Mesh, PartitionSpec as P

WAVE = ("yh", "z", "x", "c")
PEERS = ("yh", "x", "c", "lev")


def refined(mesh):
    return Mesh(mesh.devices.reshape(2, 12, 4, 2, 4), WAVE + ("lev",))


def damping_table(level_gain, wavenumbers, total_n):
    scaled = (wavenumbers * (wavenumbers + 1)).astype(jnp.float32) / jnp.float32(
        (total_n - 1) * total_n
    )
    return 1.0 / (1.0 + level_gain[:, None] * scaled[None, :] ** 2)


def on_device(
    spin_tendency,
    spreading_source,
    heat_source,
    helmholtz_inverses,
    heat_spreading_coupler,
    smoothing_strengths,
    azimuthal_order_list,
):
    rows, parts, lev_local, total_n = spreading_source.shape
    nyh, nz, nx, nc = (lax.axis_size(a) for a in WAVE)
    nlev = lax.axis_size("lev")
    peers = nyh * nx * nc
    layers = lev_local * nlev
    zero = jnp.zeros((), jnp.bfloat16)

    sent = spreading_source.reshape(rows, parts, lev_local, nlev, nyh, nz, nx, nc)
    sent = sent.transpose(4, 6, 7, 3, 5, 1, 0, 2).reshape(
        peers * nlev, nz, parts, rows * lev_local
    )
    got = lax.all_to_all(sent, PEERS, split_axis=0, concat_axis=0, tiled=True)
    matrices = lax.all_gather(helmholtz_inverses[0, 0], "z", axis=0, tiled=False)

    got = got.reshape(peers, nlev, nz, parts, rows, lev_local)
    columns = got.transpose(2, 1, 5, 0, 3, 4).reshape(nz, layers, peers * parts * rows)
    solved = jnp.einsum(
        "zkp,zpb->zkb", matrices, columns, preferred_element_type=jnp.float32
    ).astype(jnp.bfloat16)
    coupled = jnp.einsum(
        "ok,zkb->zob", heat_spreading_coupler, solved, preferred_element_type=jnp.float32
    ).astype(jnp.bfloat16)
    both = jnp.stack([solved, coupled]).reshape(2, nz, nlev, lev_local, peers, parts, rows)
    both = both.transpose(4, 2, 5, 0, 1, 6, 3).reshape(
        peers * nlev, parts, 2 * nz * rows * lev_local
    )
    back = lax.all_to_all(both, PEERS, split_axis=0, concat_axis=0, tiled=True)
    back = back.reshape(nyh, nx, nc, nlev, parts, 2, nz, rows, lev_local)
    back = back.transpose(5, 7, 4, 8, 3, 0, 6, 1, 2).reshape(
        2, rows, parts, lev_local, total_n
    )
    spreading_updated, coupled_out = back[0], back[1]

    heat_updated = (heat_source.astype(jnp.float32) - coupled_out.astype(jnp.float32)).astype(
        jnp.bfloat16
    )
    level_gain = lax.dynamic_slice_in_dim(
        smoothing_strengths, lax.axis_index("lev") * lev_local, lev_local
    )
    damping = damping_table(level_gain, jnp.arange(total_n, dtype=jnp.int32), total_n)
    spin_updated = (spin_tendency.astype(jnp.float32) * damping[None, None]).astype(jnp.bfloat16)
    interior = (
        jnp.arange(total_n, dtype=jnp.int32)[None, :] >= azimuthal_order_list[:, None]
    )[:, None, None, :]
    return (
        jnp.where(interior, spin_updated, zero),
        jnp.where(interior, spreading_updated, zero),
        jnp.where(interior, heat_updated, zero),
    )


def solution(mesh):
    spectrum = P(WAVE, None, "lev", None)
    return jax.shard_map(
        on_device,
        mesh=refined(mesh),
        in_specs=(spectrum, spectrum, spectrum, P("lev", WAVE, None, None), P(), P(), P(WAVE)),
        out_specs=(spectrum,) * 3,
        check_vma=False,
    )
```

time: 283 us -> 105 us (0.37)
  waiting for transfers between devices: 229 us -> 12.8 us
  starting transfers between devices: 7.93 us -> 30.3 us
  blocking collectives: 11 us -> 29.3 us
  local copies, waits for them, and re-layouts: 9.9 us -> 25.4 us
  between operations: 14.2 us -> 0.9 us
  matrix products: 8.56 us -> 0.67 us
  other arithmetic: 1.9 us -> 4.83 us
    all_gather x1 -> x0, waiting for transfers between devices: 214 us -> none  [on_device(): gathered = lax.all_gather(helmholtz_inverses, 'wave', axis=1, tiled=True)]
    all_gather x0 -> x1, blocking collectives: none -> 29.3 us  [on_device(): lax.all_gather(helmholtz_inverses[0, 0], 'z', axis=0, tiled=False)]
    all_to_all x1 -> x2, starting transfers between devices: 7.89 us -> 30.3 us  [the longest x1 15.8 us: on_device(): back = lax.all_to_all(both, PEERS, split_axis=0, concat_axis=0, tiled=True)]
    reshape x2 -> x8, local copies, waits for them, and re-layouts: 0.6 us -> 13.1 us  [the longest x2 7.71 us: on_device(): back = back.reshape(nyh, nx, nc, nlev, parts, 2, nz, rows, lev_local)]
    all_to_all x1 -> x0, blocking collectives: 11 us -> none  [on_device(): lax.all_to_all(spreading_source, 'lev', split_axis=3, concat_axis=2, tile...]
    dot_general x2, matrix products: 8.56 us -> 0.67 us  [the longest x1 0.4 us: on_device(): jnp.einsum('zkp,zpb->zkb', matrices, columns, preferred_element_type=jnp....]
    all_to_all x1 -> x2, waiting for transfers between devices: 14.5 us -> 12.8 us  [the longest x1 12.8 us: on_device(): back = lax.all_to_all(both, PEERS, split_axis=0, concat_axis=0, tiled=True)]
    unnamed x13 -> x20, local copies, waits for them, and re-layouts: 5.93 us -> 7.19 us
  transfers between devices with their start and end apart: 2 -> 2, of which waited for: 2 -> 1; matrix products, arithmetic and copies ran while one was open for 3% -> 2% of each run, Pallas kernels for 0% -> 0%
where the time goes in v1:
time: 105 us; the launch traced here: 104 us
  starting transfers between devices  30.3 us (29%)
  blocking collectives  29.3 us (28%)
  local copies, waits for them, and re-layouts  25.4 us (24%)
  waiting for transfers between devices  12.8 us (12%)
  other arithmetic  4.83 us (5%)
    all_gather x1, blocking collectives, on_device(): lax.all_gather(helmholtz_inverses[0, 0], 'z', axis=0, tiled=False)  29.3 us
    all_to_all x1, starting transfers between devices, on_device(): back = lax.all_to_all(both, PEERS, split_axis=0, concat_axis=0, tiled=True)  15.8 us
    all_to_all x1, starting transfers between devices, on_device(): got = lax.all_to_all(sent, PEERS, split_axis=0, concat_axis=0, tiled=True)  14.6 us
    all_to_all x1, waiting for transfers between devices, on_device(): back = lax.all_to_all(both, PEERS, split_axis=0, concat_axis=0, tiled=True)  12.8 us
    reshape x2, local copies, waits for them, and re-layouts, on_device(): back = back.reshape(nyh, nx, nc, nlev, parts, 2, nz, rows, lev_local)  7.71 us
    unnamed x20, local copies, waits for them, and re-layouts  7.19 us
    reshape x2, local copies, waits for them, and re-layouts, on_device(): both.transpose(4, 2, 5, 0, 1, 6, 3)  2.68 us
    transpose x1, other arithmetic, on_device(): both.transpose(4, 2, 5, 0, 1, 6, 3)  2.5 us
  transfers between devices with their start and end apart: 2, of which 1 were waited for; matrix products, arithmetic and copies ran while one was open for 2% of the time, Pallas kernels for 0%

profile of v1, /device:TPU:1, one launch (start us, length us, event | category | flops | bytes accessed | tf_op | source)
XLA Modules:
  0.0 104.3 jit_solution(5658772412103772768)
XLA Ops:
  0.6 1.5 %copy.42 = bf16[2,2,34,768]{2,3,1,0:T(8,128)(2,1)S(1)} copy(bf16[2,2,34,768]{3,1,2,0:T(2,128)(2,1)} %param.8) | data formatting | bytes 417792 | tf_op args[1]
  2.2 0.8 copy.58
  3.0 1.1 %reshape.100 = bf16[64,12,2,68]{3,2,1,0:T(2,128)(2,1)} reshape(bf16[2,4,2,4,12,2,2,34]{7,6,5,4,3,2,1,0:T(2,128)(2,1)S(1)} %copy.58) | data formatting | bytes 417792 | tf_op jit(solution)/shard_map/reshape | solution.py:38
  4.1 14.6 %all-to-all-start = ((bf16[64,12,2,68]{3,2,1,0:T(2,128)(2,1)}), bf16[64,12,2,68]{3,2,1,0:T(2,128)(2,1)S(1)}, u32[]{:S(2)}, u32[]{:S(2)}) async-start(bf16[64,12,2,68]{3,2,1,0:T(2,128)(2,1)} %reshape.100), calls=%async_computation | async-start | bytes 786432 | tf_op jit(solution)/shard_map/all_to_all | solution.py:41
  18.7 29.3 %all-gather = bf16[12,1,136,136]{3,2,1,0:T(8,128)(2,1)S(1)} all-gather(bf16[1,1,136,136]{3,2,1,0:T(8,128)(2,1)S(1)} %copy-done.4), channel_id=2, replica_groups=mesh['yh'=2,'z'=12,'x'=4,'c'=2,'lev'=4] {'z'}, dimensions={0}, use_global_device_ids=true | all-gather | bytes 480896 | tf_op jit(solution)/shard_map/all_gather | solution.py:42
  48.1 0.3 reshape.93
  48.5 0.3 copy.46
  48.8 0.4 reshape.94
  49.2 0.4 convolution_convert_fusion.1
  49.6 0.4 stack.9
  50.0 0.3 fusion
  50.3 0.4 stack.10
  50.7 0.6 copy.48
  51.3 0.6 copy.47
  51.9 2.5 %maximum_bitcast_fusion = bf16[16,4,2,2,12,2,34]{6,5,4,3,1,0,2:T(2,128)(2,1)S(1)} fusion(bf16[1,12,4,34,16,2,2]{3,6,1,0,2,4,5:T(2,128)(2,1)S(1)} %copy.48, bf16[1,12,4,34,16,2,2]{3,6,1,0,2,4,5:T(2,128)(2,1)S(1)} %copy.47), kind=kLoop, calls=%fused_computation | loop fusion | flops 208896 | bytes 835584 | tf_op jit(solution)/shard_map/transpose | solution.py:53
  54.4 1.5 %reshape.95 = bf16[64,2,1632]{2,0,1:T(8,128)(2,1)S(1)} reshape(bf16[16,4,2,2,12,2,34]{6,5,4,3,1,0,2:T(2,128)(2,1)S(1)} %maximum_bitcast_fusion) | data formatting | bytes 835584 | tf_op jit(solution)/shard_map/reshape | solution.py:53
  56.0 1.2 %copy.49 = bf16[64,2,1632]{2,1,0:T(2,128)(2,1)} copy(bf16[64,2,1632]{2,0,1:T(8,128)(2,1)S(1)} %reshape.95) | data formatting | bytes 835584 | tf_op jit(solution)/shard_map/reshape | solution.py:53
  57.2 15.8 %all-to-all-start.1 = ((bf16[64,2,1632]{2,1,0:T(2,128)(2,1)}), bf16[64,2,1632]{2,1,0:T(2,128)(2,1)}, u32[]{:S(2)}, u32[]{:S(2)}) async-start(bf16[64,2,1632]{2,1,0:T(2,128)(2,1)} %copy.49), calls=%async_computation.1 | async-start | bytes 851968 | tf_op jit(solution)/shard_map/all_to_all | solution.py:56
  73.1 0.9 copy.41
  74.1 0.6 copy.40
  74.7 0.6 copy.53
  75.5 12.8 %all-to-all-done.1 = bf16[64,2,1632]{2,1,0:T(2,128)(2,1)} async-done(((bf16[64,2,1632]{2,1,0:T(2,128)(2,1)}), bf16[64,2,1632]{2,1,0:T(2,128)(2,1)}, u32[]{:S(2)}, u32[]{:S(2)}) %all-to-all-start.1) | async-done | bytes 417824 | tf_op jit(solution)/shard_map/all_to_all | solution.py:56
  88.3 6.5 %reshape.101 = bf16[2,4,2,4,2,2,12,2,34]{8,7,6,5,4,3,2,1,0:T(2,128)(2,1)S(1)} reshape(bf16[64,2,1632]{2,1,0:T(2,128)(2,1)} %all-to-all-done.1) | data formatting | bytes 835584 | tf_op jit(solution)/shard_map/reshape | solution.py:57
  94.8 1.2 %copy.63 = bf16[2,4,2,4,2,2,12,2,34]{8,1,2,6,0,3,4,7,5:T(4,128)(2,1)S(1)} copy(bf16[2,4,2,4,2,2,12,2,34]{8,7,6,5,4,3,2,1,0:T(2,128)(2,1)S(1)} %reshape.101) | data formatting | bytes 835584 | tf_op jit(solution)/shard_map/reshape | solution.py:57
  96.0 0.6 slice_convert_fusion
  96.6 1.0 copy.54
  97.6 0.8 copy.52
  98.4 0.2 copy-done.1
  98.6 1.6 %fusion.3 = (bf16[2,2,34,768]{2,3,1,0:T(8,128)(2,1)S(1)}, bf16[2,2,34,768]{2,3,1,0:T(8,128)(2,1)S(1)}, bf16[2,2,34,768]{2,3,1,0:T(8,128)(2,1)}) fusion(f32[2,2,34,768]{2,3,1,0:T(8,128)S(1)} %bitcast.33, bf16[2,2,34,768]{2,3,1,0:T(8,128)(2,1)S(1)} %copy.53, pred[2,768]{1,0:T(4,128)(4,1)S(1)} %iota_compare_fusion, bf16[2,2,34,768]{2,3,1,0:T(8,128)(2,1)S(1)} %bitcast.37, ...), kind=kLoop, calls=%fused_computation.9 | loop fusion | flops 940032 | bytes 1777152 | tf_op jit(solution)/shard_map/jit(_where)/select_n | solution.py:77
  100.1 2.0 %copy.55 = bf16[2,2,34,768]{3,1,2,0:T(2,128)(2,1)} copy(bf16[2,2,34,768]{2,3,1,0:T(8,128)(2,1)} %get-tuple-element.16) | data formatting | bytes 417792
  102.2 1.1 %copy.56 = bf16[2,2,34,768]{3,1,2,0:T(2,128)(2,1)} copy(bf16[2,2,34,768]{2,3,1,0:T(8,128)(2,1)S(1)} %get-tuple-element.15) | data formatting | bytes 417792
  103.2 1.1 %copy.57 = bf16[2,2,34,768]{3,1,2,0:T(2,128)(2,1)} copy(bf16[2,2,34,768]{2,3,1,0:T(8,128)(2,1)S(1)} %get-tuple-element.14) | data formatting | bytes 417792
  (19 shorter events, 0.4 us)
Async XLA Ops:
  0.6 49.4 %copy-start = (bf16[136,136]{1,0:T(8,128)(2,1)S(1)}, bf16[136,136]{1,0:T(8,128)(2,1)}, u32[]{:S(2)}) copy-start(bf16[136,136]{1,0:T(8,128)(2,1)} %param.11) | copy-start | bytes 110980
  2.2 16.5 %copy-start.4 = (bf16[1,1,136,136]{3,2,1,0:T(8,128)(2,1)S(1)}, bf16[1,1,136,136]{3,2,1,0:T(8,128)(2,1)}, u32[]{:S(2)}) copy-start(bf16[1,1,136,136]{3,2,1,0:T(8,128)(2,1)} %param.10) | copy-start | bytes 110980
  4.1 43.9 %all-to-all-start = ((bf16[64,12,2,68]{3,2,1,0:T(2,128)(2,1)}), bf16[64,12,2,68]{3,2,1,0:T(2,128)(2,1)S(1)}, u32[]{:S(2)}, u32[]{:S(2)}) async-start(bf16[64,12,2,68]{3,2,1,0:T(2,128)(2,1)} %reshape.100), calls=%async_computation | async-start | bytes 786432 | tf_op jit(solution)/shard_map/all_to_all | solution.py:41
  54.4 18.5 %copy-start.6 = (f32[136]{0:T(256)S(1)}, f32[136]{0:T(256)}, u32[]{:S(2)}) copy-start(f32[136]{0:T(256)} %param.12) | copy-start | bytes 1636
  55.9 18.1 %copy-start.2 = (bf16[2,2,34,768]{3,1,2,0:T(2,128)(2,1)S(1)}, bf16[2,2,34,768]{3,1,2,0:T(2,128)(2,1)}, u32[]{:S(2)}) copy-start(bf16[2,2,34,768]{3,1,2,0:T(2,128)(2,1)} %param.7) | copy-start | bytes 626692
  55.9 18.8 %copy-start.3 = (bf16[2,2,34,768]{3,1,2,0:T(2,128)(2,1)S(1)}, bf16[2,2,34,768]{3,1,2,0:T(2,128)(2,1)}, u32[]{:S(2)}) copy-start(bf16[2,2,34,768]{3,1,2,0:T(2,128)(2,1)} %param.9) | copy-start | bytes 626692
  57.2 18.2 %copy-start.5 = (s32[2]{0:T(128)S(1)}, s32[2]{0:T(128)}, u32[]{:S(2)}) copy-start(s32[2]{0:T(128)} %param.13) | copy-start | bytes 28
  57.2 31.1 %all-to-all-start.1 = ((bf16[64,2,1632]{2,1,0:T(2,128)(2,1)}), bf16[64,2,1632]{2,1,0:T(2,128)(2,1)}, u32[]{:S(2)}, u32[]{:S(2)}) async-start(bf16[64,2,1632]{2,1,0:T(2,128)(2,1)} %copy.49), calls=%async_computation.1 | async-start | bytes 851968 | tf_op jit(solution)/shard_map/all_to_all | solution.py:56
  97.6 1.0 copy-start.1

commit v2 on v1

v2 whole, which is shorter than its diff:
```python
import jax
import jax.numpy as jnp
from jax import lax
from jax.experimental import pallas as pl
from jax.experimental.pallas import tpu as pltpu
from jax.sharding import Mesh, PartitionSpec as P

WAVE = ("yh", "z", "x", "c")
PEERS = ("yh", "x", "c", "lev")
NT = (((1,), (1,)), ((), ()))
NN = (((1,), (0,)), ((), ()))


def refined(mesh):
    return Mesh(mesh.devices.reshape(2, 12, 4, 2, 4), WAVE + ("lev",))


def dot(a, b, dims):
    return lax.dot_general(a, b, dims, preferred_element_type=jnp.float32)


def damping_table(level_gain, wavenumbers, total_n):
    scaled = (wavenumbers * (wavenumbers + 1)).astype(jnp.float32) / jnp.float32(
        (total_n - 1) * total_n
    )
    return 1.0 / (1.0 + level_gain[:, None] * scaled[None, :] ** 2)


def pack_kernel(m_ref, o_ref):
    m = m_ref[...].astype(jnp.float32)
    o_ref[0:136, :] = m[:, 0:128].astype(jnp.bfloat16)
    tail = m[:, 128:136]
    flipped = jnp.concatenate([tail, jnp.zeros((120, 8), jnp.float32)], axis=0)
    flipped = jnp.concatenate([flipped, jnp.zeros((256, 120), jnp.float32)], axis=1).T
    o_ref[136:152, :] = jnp.concatenate(
        [flipped[0:8, 0:128], flipped[0:8, 128:256]], axis=0
    ).astype(jnp.bfloat16)


def solve_kernel(x_ref, m_ref, c_ref, o_ref, stage):
    nz = x_ref.shape[0]
    stage[...] = jnp.zeros_like(stage)
    coupler = c_ref[...]
    for z in range(nz):
        x = x_ref[z]
        tail = m_ref[z, 136:152, :]
        x_tail = x[:, 128:136]
        low = dot(x[:, 0:128], m_ref[z, 0:136, :], NT)
        high = jnp.concatenate(
            [dot(x_tail, tail[0:8, :], NN), dot(x_tail, tail[8:16, 0:8], NN)], axis=1
        )
        solved = (low + high).astype(jnp.bfloat16)
        coupled = dot(solved, coupler, NT).astype(jnp.bfloat16)
        for f, values in enumerate((solved, coupled)):
            values = values.astype(jnp.float32)
            for c in range(2):
                for r in range(2):
                    rows = values[(c * 2 + r) * 16 : (c * 2 + r + 1) * 16, :]
                    at = z * 136 + f * 68 + r * 34
                    for l in range(4):
                        stage[l, c, :, at : at + 34] = rows[:, l * 34 : l * 34 + 34]
    for l in range(4):
        for c in range(2):
            o_ref[l, c] = stage[l, c].astype(jnp.bfloat16)


def finish_kernel(m_ref, b_ref, heat_ref, div_ref, temp_ref, stage):
    spans = []
    for c in range(2):
        flipped = b_ref[c].astype(jnp.float32).T
        spans.append([flipped[z * 136 : (z + 1) * 136, :] for z in range(12)])
    total = None
    for g in range(3):
        sides = []
        for c in range(2):
            s = spans[c][4 * g : 4 * g + 4]
            sides.append(jnp.concatenate(s, axis=1))
        left = jnp.concatenate(sides, axis=0).astype(jnp.bfloat16)
        row = lax.broadcasted_iota(jnp.int32, (256, 768), 0)
        col = lax.broadcasted_iota(jnp.int32, (256, 768), 1)
        z, s, l = 4 * g + (row >> 6), (row >> 2) & 15, row & 3
        place = l * 192 + (s >> 3) * 96 + z * 8 + (s & 7)
        put = jnp.where(col == place, 1.0, 0.0).astype(jnp.bfloat16)
        part = dot(left, put, NN)
        total = part if total is None else total + part
    for c in range(2):
        for t in range(6):
            stage[t, pl.ds(c, 136, 2), :] = total[
                c * 136 : (c + 1) * 136, t * 128 : (t + 1) * 128
            ]
    lane = lax.broadcasted_iota(jnp.int32, (2, 768), 1)
    for r in range(2):
        inside = lane >= m_ref[r]
        for k in range(34):
            at = 2 * (r * 34 + k)
            solved, coupled = (
                jnp.concatenate([stage[t, i : i + 2, :] for t in range(6)], axis=1)
                for i in (at, 136 + at)
            )
            heat = heat_ref[r, k].astype(jnp.float32)
            div_ref[r, k] = jnp.where(inside, solved, 0.0).astype(jnp.bfloat16)
            temp_ref[r, k] = jnp.where(inside, heat - coupled, 0.0).astype(jnp.bfloat16)


def vmem(n):
    return [pl.BlockSpec(memory_space=pltpu.VMEM)] * n


def on_device(
    spin_tendency,
    spreading_source,
    heat_source,
    helmholtz_inverses,
    heat_spreading_coupler,
    smoothing_strengths,
    azimuthal_order_list,
):
    rows, parts, lev_local, total_n = spreading_source.shape
    nyh, nz, nx, nc = (lax.axis_size(a) for a in WAVE)
    nlev = lax.axis_size("lev")
    peers = nyh * nx * nc
    layers = lev_local * nlev
    zero = jnp.zeros((), jnp.bfloat16)

    packed = pl.pallas_call(
        pack_kernel,
        out_shape=jax.ShapeDtypeStruct((layers + 16, 128), jnp.bfloat16),
        in_specs=vmem(1),
        out_specs=vmem(1)[0],
    )(helmholtz_inverses[0, 0])

    sent = spreading_source.reshape(rows, parts, lev_local, nlev, nyh, nz, nx, nc)
    sent = sent.transpose(4, 6, 7, 3, 5, 1, 0, 2).reshape(
        peers * nlev, nz, parts, rows * lev_local
    )
    got = lax.all_to_all(sent, PEERS, split_axis=0, concat_axis=0, tiled=True)
    matrices = lax.all_gather(packed, "z", axis=0, tiled=False)

    got = got.reshape(peers, nlev, nz, parts, rows, lev_local)
    columns = got.transpose(2, 3, 4, 0, 1, 5).reshape(nz, parts * rows * peers, layers)
    width = 13 * 128
    both = pl.pallas_call(
        solve_kernel,
        out_shape=jax.ShapeDtypeStruct((nlev, parts, peers, width), jnp.bfloat16),
        in_specs=vmem(3),
        out_specs=vmem(1)[0],
        scratch_shapes=[pltpu.VMEM((nlev, parts, peers, width), jnp.float32)],
    )(columns, matrices, heat_spreading_coupler)
    both = both.transpose(2, 0, 1, 3).reshape(peers * nlev, parts, width)
    back = lax.all_to_all(both, PEERS, split_axis=0, concat_axis=0, tiled=True)
    back = back.transpose(1, 0, 2)

    out = jax.ShapeDtypeStruct((rows, lev_local, parts, total_n), jnp.bfloat16)
    divergence, temperature = pl.pallas_call(
        finish_kernel,
        out_shape=(out, out),
        in_specs=[pl.BlockSpec(memory_space=pltpu.SMEM)] + vmem(2),
        out_specs=tuple(vmem(2)),
        scratch_shapes=[pltpu.VMEM((total_n // 128, 4 * rows * lev_local, 128), jnp.float32)],
    )(azimuthal_order_list, back, heat_source.transpose(0, 2, 1, 3))

    level_gain = lax.dynamic_slice_in_dim(
        smoothing_strengths, lax.axis_index("lev") * lev_local, lev_local
    )
    damping = damping_table(level_gain, jnp.arange(total_n, dtype=jnp.int32), total_n)
    spin_updated = (spin_tendency.astype(jnp.float32) * damping[None, None]).astype(jnp.bfloat16)
    interior = (
        jnp.arange(total_n, dtype=jnp.int32)[None, :] >= azimuthal_order_list[:, None]
    )[:, None, None, :]
    return (
        jnp.where(interior, spin_updated, zero),
        divergence.transpose(0, 2, 1, 3),
        temperature.transpose(0, 2, 1, 3),
    )


def solution(mesh):
    spectrum = P(WAVE, None, "lev", None)
    return jax.shard_map(
        on_device,
        mesh=refined(mesh),
        in_specs=(spectrum, spectrum, spectrum, P("lev", WAVE, None, None), P(), P(), P(WAVE)),
        out_specs=(spectrum,) * 3,
        check_vma=False,
    )
```

time: 105 us -> 92.1 us (0.88)
  local copies, waits for them, and re-layouts: 25.4 us -> 9.64 us
  Pallas kernels: 0 us -> 8.55 us
  other arithmetic: 4.83 us -> 1.08 us
    reshape x5 -> x1, local copies, waits for them, and re-layouts: 10.8 us -> 1.19 us  [on_device(): got.transpose(2, 3, 4, 0, 1, 5).reshape(nz, parts * rows * peers, layers)]
    pallas_call x0 -> x3, Pallas kernels: none -> 8.55 us  [the longest x1 3.84 us: on_device(): pl.pallas_call(solve_kernel, out_shape=jax.ShapeDtypeStruct((nlev, parts,...]
    unnamed x20 -> x7, local copies, waits for them, and re-layouts: 7.19 us -> 2.82 us
    transpose x1 -> x0, other arithmetic: 2.5 us -> none  [on_device(): both.transpose(4, 2, 5, 0, 1, 6, 3)]
    transpose x1 -> x2, local copies, waits for them, and re-layouts: 0.33 us -> 2.46 us  [the longest x1 2.08 us: on_device(): both = both.transpose(2, 0, 1, 3).reshape(peers * nlev, parts, width)]
    another operation x4 -> x0, local copies, waits for them, and re-layouts: 1.98 us -> none  [on_device(): jnp.stack([solved, coupled])]
  transfers between devices with their start and end apart: 2 -> 2, of which waited for: 1 -> 1; matrix products, arithmetic and copies ran while one was open for 2% -> 1% of each run, Pallas kernels for 0% -> 2%
where the time goes in v2:
time: 92.1 us; the launch traced here: 91.7 us
  starting transfers between devices  29.7 us (32%)
  blocking collectives  29.1 us (32%)
  waiting for transfers between devices  12.9 us (14%)
  local copies, waits for them, and re-layouts  9.64 us (10%)
  Pallas kernels  8.55 us (9%)
  other arithmetic  1.08 us (1%)
    all_gather x1, blocking collectives, on_device(): matrices = lax.all_gather(packed, 'z', axis=0, tiled=False)  29.1 us
    all_to_all x1, starting transfers between devices, on_device(): back = lax.all_to_all(both, PEERS, split_axis=0, concat_axis=0, tiled=True)  15.1 us
    all_to_all x1, starting transfers between devices, on_device(): got = lax.all_to_all(sent, PEERS, split_axis=0, concat_axis=0, tiled=True)  14.6 us
    all_to_all x1, waiting for transfers between devices, on_device(): back = lax.all_to_all(both, PEERS, split_axis=0, concat_axis=0, tiled=True)  12.9 us
    pallas_call x1, Pallas kernels, on_device(): pl.pallas_call(solve_kernel, out_shape=jax.ShapeDtypeStruct((nlev, parts,...  3.84 us
    pallas_call x1, Pallas kernels, on_device(): pl.pallas_call(finish_kernel, out_shape=(out, out), in_specs=[pl.BlockSpe...  3.14 us
    unnamed x7, local copies, waits for them, and re-layouts  2.82 us
    transpose x1, local copies, waits for them, and re-layouts, on_device(): both = both.transpose(2, 0, 1, 3).reshape(peers * nlev, parts, width)  2.08 us
  transfers between devices with their start and end apart: 2, of which 1 were waited for; matrix products, arithmetic and copies ran while one was open for 1% of the time, Pallas kernels for 2%

profile of v2, /device:TPU:1, one launch (start us, length us, event | category | flops | bytes accessed | tf_op | source)
XLA Modules:
  0.0 91.7 jit_solution(9539498366656034155)
XLA Ops:
  0.6 1.5 %copy.21 = bf16[2,2,34,768]{2,3,1,0:T(8,128)(2,1)S(1)} copy(bf16[2,2,34,768]{3,1,2,0:T(2,128)(2,1)} %param.8) | data formatting | bytes 417792 | tf_op args[1]
  2.1 0.8 copy.28
  2.9 1.1 %reshape.82 = bf16[64,12,2,68]{3,2,1,0:T(2,128)(2,1)} reshape(bf16[2,4,2,4,12,2,2,34]{7,6,5,4,3,2,1,0:T(2,128)(2,1)S(1)} %copy.28) | data formatting | bytes 417792 | tf_op jit(solution)/shard_map/reshape | solution.py:133
  4.0 14.6 %all-to-all-start = ((bf16[64,12,2,68]{3,2,1,0:T(2,128)(2,1)}), bf16[64,12,2,68]{3,2,1,0:T(2,128)(2,1)S(1)}, u32[]{:S(2)}, u32[]{:S(2)}) async-start(bf16[64,12,2,68]{3,2,1,0:T(2,128)(2,1)} %reshape.82), calls=%async_computation | async-start | bytes 786432 | tf_op jit(solution)/shard_map/all_to_all | solution.py:136
  18.6 1.6 %shard_map.94 = bf16[152,128]{1,0:T(8,128)(2,1)} custom-call(bf16[136,136]{1,0:T(8,128)(2,1)} %bitcast.24), custom_call_target="tpu_custom_call" | custom-call | tf_op jit(solution)/shard_map/pallas_call | solution.py:125
  20.2 29.1 %all-gather = bf16[1824,128]{1,0:T(8,128)(2,1)} all-gather(bf16[152,128]{1,0:T(8,128)(2,1)} %shard_map.94), channel_id=2, replica_groups=mesh['yh'=2,'z'=12,'x'=4,'c'=2,'lev'=4] {'z'}, dimensions={0}, use_global_device_ids=true | all-gather | bytes 505856 | tf_op jit(solution)/shard_map/all_gather | solution.py:137
  49.3 0.0 all-to-all-done
  49.3 0.1 copy.24
  49.4 0.3 reshape.78
  49.7 0.4 copy.25
  50.1 1.2 %reshape.79.x_ref = bf16[12,64,136]{2,1,0:T(8,128)(2,1)} reshape(bf16[12,2,2,16,4,34]{5,4,3,2,1,0:T(4,128)(2,1)S(1)} %copy.25) | data formatting | bytes 417792 | tf_op jit(solution)/shard_map/reshape | solution.py:140
  51.3 3.8 %shard_map.95 = bf16[4,2,16,1664]{3,2,1,0:T(8,128)(2,1)} custom-call(bf16[12,64,136]{2,1,0:T(8,128)(2,1)} %reshape.79.x_ref, bf16[12,152,128]{2,1,0:T(8,128)(2,1)} %bitcast.20, bf16[136,136]{1,0:T(8,128)(2,1)} %c_ref.1), custom_call_target="tpu_custom_call" | custom-call | tf_op jit(solution)/shard_map/pallas_call | solution.py:142
  55.1 2.1 %copy.26 = bf16[16,4,2,1664]{3,2,1,0:T(2,128)(2,1)} copy(bf16[16,4,2,1664]{3,0,2,1:T(8,128)(2,1)} %bitcast.22) | data formatting | bytes 851968 | tf_op jit(solution)/shard_map/transpose | solution.py:149
  57.2 0.0 copy-start
  57.2 15.1 %all-to-all-start.1 = ((bf16[64,2,1664]{2,1,0:T(2,128)(2,1)}), bf16[64,2,1664]{2,1,0:T(2,128)(2,1)S(1)}, u32[]{:S(2)}, u32[]{:S(2)}) async-start(bf16[64,2,1664]{2,1,0:T(2,128)(2,1)} %bitcast.6), calls=%async_computation.1 | async-start | bytes 851968 | tf_op jit(solution)/shard_map/all_to_all | solution.py:150
  72.4 0.0 copy-start.2
  72.4 0.7 copy-done.2
  73.0 0.1 dynamic_slice.3
  73.1 0.0 copy-start.1
  73.1 0.6 copy-done.1
  73.8 0.1 iota_compare_fusion
  73.8 0.1 add_divide_fusion
  73.9 0.0 copy-done
  73.9 0.9 broadcast_select_fusion
  74.9 12.9 %all-to-all-done.1 = bf16[64,2,1664]{2,1,0:T(2,128)(2,1)S(1)} async-done(((bf16[64,2,1664]{2,1,0:T(2,128)(2,1)}), bf16[64,2,1664]{2,1,0:T(2,128)(2,1)S(1)}, u32[]{:S(2)}, u32[]{:S(2)}) %all-to-all-start.1) | async-done | bytes 426016 | tf_op jit(solution)/shard_map/all_to_all | solution.py:150
  87.8 0.8 copy.31
  88.6 3.1 %shard_map.96 = (bf16[2,34,2,768]{3,2,1,0:T(2,128)(2,1)}, bf16[2,34,2,768]{3,2,1,0:T(2,128)(2,1)}) custom-call(s32[2]{0:T(128)} %m_ref.1, bf16[2,64,1664]{2,1,0:T(8,128)(2,1)} %bitcast.21, bf16[2,34,2,768]{3,2,1,0:T(2,128)(2,1)} %bitcast.23), custom_call_target="tpu_custom_call" | custom-call | tf_op jit(solution)/shard_map/pallas_call | solution.py:154
  (1 shorter events, 0.0 us)
Async XLA Ops:
  4.0 45.2 %all-to-all-start = ((bf16[64,12,2,68]{3,2,1,0:T(2,128)(2,1)}), bf16[64,12,2,68]{3,2,1,0:T(2,128)(2,1)S(1)}, u32[]{:S(2)}, u32[]{:S(2)}) async-start(bf16[64,12,2,68]{3,2,1,0:T(2,128)(2,1)} %reshape.82), calls=%async_computation | async-start | bytes 786432 | tf_op jit(solution)/shard_map/all_to_all | solution.py:136
  57.2 16.7 %copy-start = (bf16[2,2,34,768]{3,1,2,0:T(2,128)(2,1)S(1)}, bf16[2,2,34,768]{3,1,2,0:T(2,128)(2,1)}, u32[]{:S(2)}) copy-start(bf16[2,2,34,768]{3,1,2,0:T(2,128)(2,1)} %param.7) | copy-start | bytes 626692
  57.2 30.6 %all-to-all-start.1 = ((bf16[64,2,1664]{2,1,0:T(2,128)(2,1)}), bf16[64,2,1664]{2,1,0:T(2,128)(2,1)S(1)}, u32[]{:S(2)}, u32[]{:S(2)}) async-start(bf16[64,2,1664]{2,1,0:T(2,128)(2,1)} %bitcast.6), calls=%async_computation.1 | async-start | bytes 851968 | tf_op jit(solution)/shard_map/all_to_all | solution.py:150
  72.4 0.7 copy-start.2
  73.1 0.7 copy-start.1

commit v3 on v2

--- a/solution.py
+++ b/solution.py
@@ -9,6 +9,7 @@
 PEERS = ("yh", "x", "c", "lev")
 NT = (((1,), (1,)), ((), ()))
 NN = (((1,), (0,)), ((), ()))
+LIMIT = pltpu.CompilerParams(vmem_limit_bytes=16 * 2**20)
 
 
 def refined(mesh):
@@ -26,7 +27,7 @@
     return 1.0 / (1.0 + level_gain[:, None] * scaled[None, :] ** 2)
 
 
-def pack_kernel(m_ref, o_ref):
+def pack_matrix(m_ref, o_ref):
     m = m_ref[...].astype(jnp.float32)
     o_ref[0:136, :] = m[:, 0:128].astype(jnp.bfloat16)
     tail = m[:, 128:136]
@@ -37,44 +38,78 @@
     ).astype(jnp.bfloat16)
 
 
-def solve_kernel(x_ref, m_ref, c_ref, o_ref, stage):
-    nz = x_ref.shape[0]
-    stage[...] = jnp.zeros_like(stage)
-    coupler = c_ref[...]
+def prepare_kernel(x_ref, m_ref, o_ref, p_ref):
+    pack_matrix(m_ref, p_ref)
+    x = x_ref[...].astype(jnp.float32)
+    sides = []
+    for c in range(2):
+        rows = jnp.concatenate(
+            [x[0, :, c, :], x[1, :, c, :], jnp.zeros((4, 768), jnp.float32)], axis=0
+        )
+        sides.append(rows.T[:, 0:68])
+    both = jnp.stack(sides, axis=1).astype(jnp.bfloat16).reshape(4, 2, 12, 8, 2, 68)
+    for l in range(4):
+        for yh in range(2):
+            for z in range(12):
+                o_ref[yh, :, l, z] = both[l, yh, z]
+
+
+def solve_kernel(x_ref, m_ref, c_ref, o_ref, stage, sol):
+    nz = m_ref.shape[0]
+    for l in range(4):
+        for c in range(2):
+            stage[l, c, :, 1536:1664] = jnp.zeros((16, 128), jnp.float32)
     for z in range(nz):
-        x = x_ref[z]
+        parts = ([], [])
+        for l in range(4):
+            got = x_ref[:, l, z].astype(jnp.float32)
+            for c in range(2):
+                parts[c].append(got[:, c, :])
+        x = jnp.concatenate(
+            [
+                jnp.concatenate(
+                    [parts[c][l][:, r * 34 : r * 34 + 34] for l in range(4)], axis=1
+                )
+                for c in range(2)
+                for r in range(2)
+            ],
+            axis=0,
+        ).astype(jnp.bfloat16)
         tail = m_ref[z, 136:152, :]
         x_tail = x[:, 128:136]
         low = dot(x[:, 0:128], m_ref[z, 0:136, :], NT)
         high = jnp.concatenate(
             [dot(x_tail, tail[0:8, :], NN), dot(x_tail, tail[8:16, 0:8], NN)], axis=1
         )
-        solved = (low + high).astype(jnp.bfloat16)
-        coupled = dot(solved, coupler, NT).astype(jnp.bfloat16)
-        for f, values in enumerate((solved, coupled)):
-            values = values.astype(jnp.float32)
-            for c in range(2):
-                for r in range(2):
-                    rows = values[(c * 2 + r) * 16 : (c * 2 + r + 1) * 16, :]
-                    at = z * 136 + f * 68 + r * 34
-                    for l in range(4):
-                        stage[l, c, :, at : at + 34] = rows[:, l * 34 : l * 34 + 34]
+        sol[z * 64 : z * 64 + 64, :] = (low + high).astype(jnp.bfloat16)
+    coupled = dot(sol[...], c_ref[...], NT).astype(jnp.bfloat16)
+    for z in range(nz):
+        both = [
+            values[z * 64 : z * 64 + 64, :].astype(jnp.float32) for values in (sol, coupled)
+        ]
+        for c in range(2):
+            for l in range(4):
+                stage[l, c, :, z * 136 : z * 136 + 136] = jnp.concatenate(
+                    [
+                        values[(c * 2 + r) * 16 : (c * 2 + r) * 16 + 16, l * 34 : l * 34 + 34]
+                        for values in both
+                        for r in range(2)
+                    ],
+                    axis=1,
+                )
     for l in range(4):
-        for c in range(2):
-            o_ref[l, c] = stage[l, c].astype(jnp.bfloat16)
+        o_ref[:, l] = jnp.stack([stage[l, 0], stage[l, 1]], axis=1).astype(jnp.bfloat16)
 
 
 def finish_kernel(m_ref, b_ref, heat_ref, div_ref, temp_ref, stage):
+    full = b_ref[...].astype(jnp.float32)
     spans = []
     for c in range(2):
-        flipped = b_ref[c].astype(jnp.float32).T
+        flipped = full[:, c, :].T
         spans.append([flipped[z * 136 : (z + 1) * 136, :] for z in range(12)])
     total = None
     for g in range(3):
-        sides = []
-        for c in range(2):
-            s = spans[c][4 * g : 4 * g + 4]
-            sides.append(jnp.concatenate(s, axis=1))
+        sides = [jnp.concatenate(spans[c][4 * g : 4 * g + 4], axis=1) for c in range(2)]
         left = jnp.concatenate(sides, axis=0).astype(jnp.bfloat16)
         row = lax.broadcasted_iota(jnp.int32, (256, 768), 0)
         col = lax.broadcasted_iota(jnp.int32, (256, 768), 1)
@@ -122,33 +157,38 @@
     layers = lev_local * nlev
     zero = jnp.zeros((), jnp.bfloat16)
 
-    packed = pl.pallas_call(
-        pack_kernel,
-        out_shape=jax.ShapeDtypeStruct((layers + 16, 128), jnp.bfloat16),
-        in_specs=vmem(1),
-        out_specs=vmem(1)[0],
-    )(helmholtz_inverses[0, 0])
-
-    sent = spreading_source.reshape(rows, parts, lev_local, nlev, nyh, nz, nx, nc)
-    sent = sent.transpose(4, 6, 7, 3, 5, 1, 0, 2).reshape(
-        peers * nlev, nz, parts, rows * lev_local
-    )
+    sent, packed = pl.pallas_call(
+        prepare_kernel,
+        out_shape=(
+            jax.ShapeDtypeStruct((nyh, nx * nc, nlev, nz, parts, rows * lev_local), jnp.bfloat16),
+            jax.ShapeDtypeStruct((layers + 16, 128), jnp.bfloat16),
+        ),
+        in_specs=vmem(2),
+        out_specs=tuple(vmem(2)),
+        compiler_params=LIMIT,
+    )(spreading_source.transpose(0, 2, 1, 3), helmholtz_inverses[0, 0])
+    sent = sent.reshape(peers * nlev, nz, parts, rows * lev_local)
     got = lax.all_to_all(sent, PEERS, split_axis=0, concat_axis=0, tiled=True)
     matrices = lax.all_gather(packed, "z", axis=0, tiled=False)
 
-    got = got.reshape(peers, nlev, nz, parts, rows, lev_local)
-    columns = got.transpose(2, 3, 4, 0, 1, 5).reshape(nz, parts * rows * peers, layers)
     width = 13 * 128
     both = pl.pallas_call(
         solve_kernel,
-        out_shape=jax.ShapeDtypeStruct((nlev, parts, peers, width), jnp.bfloat16),
+        out_shape=jax.ShapeDtypeStruct((peers, nlev, parts, width), jnp.bfloat16),
         in_specs=vmem(3),
         out_specs=vmem(1)[0],
-        scratch_shapes=[pltpu.VMEM((nlev, parts, peers, width), jnp.float32)],
-    )(columns, matrices, heat_spreading_coupler)
-    both = both.transpose(2, 0, 1, 3).reshape(peers * nlev, parts, width)
+        scratch_shapes=[
+            pltpu.VMEM((nlev, parts, peers, width), jnp.float32),
+            pltpu.VMEM((nz * parts * rows * peers, layers), jnp.bfloat16),
+        ],
+        compiler_params=LIMIT,
+    )(
+        got.reshape(peers, nlev, nz, parts, rows * lev_local),
+        matrices,
+        heat_spreading_coupler,
+    )
+    both = both.reshape(peers * nlev, parts, width)
     back = lax.all_to_all(both, PEERS, split_axis=0, concat_axis=0, tiled=True)
-    back = back.transpose(1, 0, 2)
 
     out = jax.ShapeDtypeStruct((rows, lev_local, parts, total_n), jnp.bfloat16)
     divergence, temperature = pl.pallas_call(
@@ -157,6 +197,7 @@
         in_specs=[pl.BlockSpec(memory_space=pltpu.SMEM)] + vmem(2),
         out_specs=tuple(vmem(2)),
         scratch_shapes=[pltpu.VMEM((total_n // 128, 4 * rows * lev_local, 128), jnp.float32)],
+        compiler_params=LIMIT,
     )(azimuthal_order_list, back, heat_source.transpose(0, 2, 1, 3))
 
     level_gain = lax.dynamic_slice_in_dim(

time: 92.1 us -> 83.1 us (0.902)
  local copies, waits for them, and re-layouts: 9.64 us -> 3.22 us
  blocking collectives: 29.1 us -> 27.7 us
    reshape x4 -> x0, local copies, waits for them, and re-layouts: 3.43 us -> none  [the longest x2 1.91 us: on_device(): sent.transpose(4, 6, 7, 3, 5, 1, 0, 2)]
    transpose x2 -> x0, local copies, waits for them, and re-layouts: 2.46 us -> none  [the longest x1 2.08 us: on_device(): both = both.transpose(2, 0, 1, 3).reshape(peers * nlev, parts, width)]
    all_gather x1, blocking collectives: 29.1 us -> 27.7 us  [on_device(): matrices = lax.all_gather(packed, 'z', axis=0, tiled=False)]
    unnamed x7 -> x14, local copies, waits for them, and re-layouts: 2.82 us -> 3.14 us
  transfers between devices with their start and end apart: 2 -> 2, of which waited for: 1 -> 1; matrix products, arithmetic and copies ran while one was open for 1% -> 1% of each run, Pallas kernels for 2% -> 0%
where the time goes in v3:
time: 83.1 us; the launch traced here: 82.7 us
  starting transfers between devices  29.5 us (35%)
  blocking collectives  27.7 us (33%)
  waiting for transfers between devices  12.9 us (16%)
  Pallas kernels  7.63 us (9%)
  local copies, waits for them, and re-layouts  3.22 us (4%)
  other arithmetic  1.08 us (1%)
    all_gather x1, blocking collectives, on_device(): matrices = lax.all_gather(packed, 'z', axis=0, tiled=False)  27.7 us
    all_to_all x1, starting transfers between devices, on_device(): back = lax.all_to_all(both, PEERS, split_axis=0, concat_axis=0, tiled=True)  14.9 us
    all_to_all x1, starting transfers between devices, on_device(): got = lax.all_to_all(sent, PEERS, split_axis=0, concat_axis=0, tiled=True)  14.6 us
    all_to_all x1, waiting for transfers between devices, on_device(): back = lax.all_to_all(both, PEERS, split_axis=0, concat_axis=0, tiled=True)  12.9 us
    pallas_call x1, Pallas kernels, on_device(): pl.pallas_call(solve_kernel, out_shape=jax.ShapeDtypeStruct((peers, nlev,...  3.24 us
    unnamed x14, local copies, waits for them, and re-layouts  3.14 us
    pallas_call x1, Pallas kernels, on_device(): pl.pallas_call(finish_kernel, out_shape=(out, out), in_specs=[pl.BlockSpe...  2.8 us
  transfers between devices with their start and end apart: 2, of which 1 were waited for; matrix products, arithmetic and copies ran while one was open for 1% of the time, Pallas kernels for 0%

profile of v3, /device:TPU:1, one launch (start us, length us, event | category | flops | bytes accessed | tf_op | source)
XLA Modules:
  0.0 82.7 jit_solution(4275996261018448459)
XLA Ops:
  0.6 0.0 copy-start.1
  0.6 0.9 %copy-done.1 = bf16[2,2,34,768]{3,1,2,0:T(2,128)(2,1)S(1)} copy-done((bf16[2,2,34,768]{3,1,2,0:T(2,128)(2,1)S(1)}, bf16[2,2,34,768]{3,1,2,0:T(2,128)(2,1)}, u32[]{:S(2)}) %copy-start.1) | copy-done | bytes 208920
  1.6 0.0 copy-start.2
  1.6 0.9 %copy-done.2 = bf16[1,1,136,136]{3,2,1,0:T(8,128)(2,1)S(1)} copy-done((bf16[1,1,136,136]{3,2,1,0:T(8,128)(2,1)S(1)}, bf16[1,1,136,136]{3,2,1,0:T(8,128)(2,1)}, u32[]{:S(2)}) %copy-start.2) | copy-done | bytes 37016
  2.4 1.6 %shard_map.94 = (bf16[2,8,4,12,2,68]{5,4,3,2,1,0:T(2,128)(2,1)}, bf16[152,128]{1,0:T(8,128)(2,1)S(1)}) custom-call(bf16[2,34,2,768]{3,2,1,0:T(2,128)(2,1)S(1)} %bitcast.12, bf16[136,136]{1,0:T(8,128)(2,1)S(1)} %bitcast.13), custom_call_target="tpu_custom_call" | custom-call | tf_op jit(solution)/shard_map/pallas_call | solution.py:160
  4.0 14.6 %all-to-all-start = ((bf16[64,12,2,68]{3,2,1,0:T(2,128)(2,1)}), bf16[64,12,2,68]{3,2,1,0:T(2,128)(2,1)S(1)}, u32[]{:S(2)}, u32[]{:S(2)}) async-start(bf16[64,12,2,68]{3,2,1,0:T(2,128)(2,1)} %bitcast.2), calls=%async_computation | async-start | bytes 786432 | tf_op jit(solution)/shard_map/all_to_all | solution.py:171
  18.6 0.0 copy-start.3
  18.6 27.7 %all-gather = bf16[1824,128]{1,0:T(8,128)(2,1)S(1)} all-gather(bf16[152,128]{1,0:T(8,128)(2,1)S(1)} %get-tuple-element.8), channel_id=2, replica_groups=mesh['yh'=2,'z'=12,'x'=4,'c'=2,'lev'=4] {'z'}, dimensions={0}, use_global_device_ids=true | all-gather | bytes 505856 | tf_op jit(solution)/shard_map/all_gather | solution.py:172
  46.3 0.0 all-to-all-done
  46.3 0.0 copy-done.3
  46.3 3.2 %shard_map.95 = bf16[16,4,2,1664]{3,2,1,0:T(2,128)(2,1)} custom-call(bf16[16,4,12,2,68]{4,3,2,1,0:T(2,128)(2,1)S(1)} %bitcast.10, bf16[12,152,128]{2,1,0:T(8,128)(2,1)S(1)} %bitcast.9, bf16[136,136]{1,0:T(8,128)(2,1)S(1)} %copy-done.3), custom_call_target="tpu_custom_call" | custom-call | tf_op jit(solution)/shard_map/pallas_call | solution.py:175
  49.6 0.0 copy-start.5
  49.6 14.9 %all-to-all-start.1 = ((bf16[64,2,1664]{2,1,0:T(2,128)(2,1)}), bf16[64,2,1664]{2,1,0:T(2,128)(2,1)S(1)}, u32[]{:S(2)}, u32[]{:S(2)}) async-start(bf16[64,2,1664]{2,1,0:T(2,128)(2,1)} %bitcast.5), calls=%async_computation.1 | async-start | bytes 851968 | tf_op jit(solution)/shard_map/all_to_all | solution.py:191
  64.5 0.0 copy-start.6
  64.5 0.7 copy-done.6
  65.2 0.1 dynamic_slice.3
  65.3 0.0 copy-start.4
  65.3 0.6 copy-done.4
  65.9 0.1 iota_compare_fusion
  66.0 0.1 add_divide_fusion
  66.1 0.0 copy-done.5
  66.1 0.0 copy-start
  66.1 0.9 %broadcast_select_fusion = bf16[2,2,34,768]{3,1,2,0:T(2,128)(2,1)} fusion(pred[2,768]{1,0:T(4,128)(4,1)S(1)} %iota_compare_fusion, bf16[2,2,34,768]{3,1,2,0:T(2,128)(2,1)S(1)} %copy-done.5, f32[34,768]{1,0:T(8,128)S(1)} %add_divide_fusion), kind=kLoop, calls=%fused_computation.1 | loop fusion | flops 417792 | bytes 523776 | tf_op jit(solution)/shard_map/jit(_where)/select_n | solution.py:212
  67.0 12.9 %all-to-all-done.1.b_ref = bf16[64,2,1664]{2,1,0:T(2,128)(2,1)S(1)} async-done(((bf16[64,2,1664]{2,1,0:T(2,128)(2,1)}), bf16[64,2,1664]{2,1,0:T(2,128)(2,1)S(1)}, u32[]{:S(2)}, u32[]{:S(2)}) %all-to-all-start.1) | async-done | bytes 426016 | tf_op jit(solution)/shard_map/all_to_all | solution.py:191
  79.9 0.0 copy-done
  79.9 2.8 %shard_map.96 = (bf16[2,34,2,768]{3,2,1,0:T(2,128)(2,1)}, bf16[2,34,2,768]{3,2,1,0:T(2,128)(2,1)}) custom-call(s32[2]{0:T(128)S(1)} %copy-done.4, bf16[64,2,1664]{2,1,0:T(2,128)(2,1)S(1)} %all-to-all-done.1.b_ref, bf16[2,34,2,768]{3,2,1,0:T(2,128)(2,1)S(1)} %bitcast.11), custom_call_target="tpu_custom_call" | custom-call | tf_op jit(solution)/shard_map/pallas_call | solution.py:194
  (1 shorter events, 0.0 us)
Async XLA Ops:
  0.6 0.9 %copy-start.1 = (bf16[2,2,34,768]{3,1,2,0:T(2,128)(2,1)S(1)}, bf16[2,2,34,768]{3,1,2,0:T(2,128)(2,1)}, u32[]{:S(2)}) copy-start(bf16[2,2,34,768]{3,1,2,0:T(2,128)(2,1)} %param.8) | copy-start | bytes 626692
  1.6 0.9 %copy-start.2 = (bf16[1,1,136,136]{3,2,1,0:T(8,128)(2,1)S(1)}, bf16[1,1,136,136]{3,2,1,0:T(8,128)(2,1)}, u32[]{:S(2)}) copy-start(bf16[1,1,136,136]{3,2,1,0:T(8,128)(2,1)} %param.10) | copy-start | bytes 110980
  4.0 42.3 %all-to-all-start = ((bf16[64,12,2,68]{3,2,1,0:T(2,128)(2,1)}), bf16[64,12,2,68]{3,2,1,0:T(2,128)(2,1)S(1)}, u32[]{:S(2)}, u32[]{:S(2)}) async-start(bf16[64,12,2,68]{3,2,1,0:T(2,128)(2,1)} %bitcast.2), calls=%async_computation | async-start | bytes 786432 | tf_op jit(solution)/shard_map/all_to_all | solution.py:171
  18.6 27.7 %copy-start.3 = (bf16[136,136]{1,0:T(8,128)(2,1)S(1)}, bf16[136,136]{1,0:T(8,128)(2,1)}, u32[]{:S(2)}) copy-start(bf16[136,136]{1,0:T(8,128)(2,1)} %c_ref.1) | copy-start | bytes 110980
  49.6 16.5 %copy-start.5 = (bf16[2,2,34,768]{3,1,2,0:T(2,128)(2,1)S(1)}, bf16[2,2,34,768]{3,1,2,0:T(2,128)(2,1)}, u32[]{:S(2)}) copy-start(bf16[2,2,34,768]{3,1,2,0:T(2,128)(2,1)} %param.7) | copy-start | bytes 626692
  49.6 30.3 %all-to-all-start.1 = ((bf16[64,2,1664]{2,1,0:T(2,128)(2,1)}), bf16[64,2,1664]{2,1,0:T(2,128)(2,1)S(1)}, u32[]{:S(2)}, u32[]{:S(2)}) async-start(bf16[64,2,1664]{2,1,0:T(2,128)(2,1)} %bitcast.5), calls=%async_computation.1 | async-start | bytes 851968 | tf_op jit(solution)/shard_map/all_to_all | solution.py:191
  64.5 0.7 copy-start.6
  65.3 0.7 copy-start.4
  66.1 13.8 %copy-start = (bf16[2,2,34,768]{3,1,2,0:T(2,128)(2,1)S(1)}, bf16[2,2,34,768]{3,1,2,0:T(2,128)(2,1)}, u32[]{:S(2)}) copy-start(bf16[2,2,34,768]{3,1,2,0:T(2,128)(2,1)} %param.9) | copy-start | bytes 626692

commit v4 on v3

--- a/solution.py
+++ b/solution.py
@@ -5,15 +5,16 @@
 from jax.experimental.pallas import tpu as pltpu
 from jax.sharding import Mesh, PartitionSpec as P
 
-WAVE = ("yh", "z", "x", "c")
-PEERS = ("yh", "x", "c", "lev")
+WAVE = ("yh", "zh", "zl", "x", "c")
+PEERS = ("yh", "zl", "x", "lev")
+SHARERS = ("zh", "c")
 NT = (((1,), (1,)), ((), ()))
 NN = (((1,), (0,)), ((), ()))
 LIMIT = pltpu.CompilerParams(vmem_limit_bytes=16 * 2**20)
 
 
 def refined(mesh):
-    return Mesh(mesh.devices.reshape(2, 12, 4, 2, 4), WAVE + ("lev",))
+    return Mesh(mesh.devices.reshape(2, 6, 2, 4, 2, 4), WAVE + ("lev",))
 
 
 def dot(a, b, dims):
@@ -38,23 +39,40 @@
     ).astype(jnp.bfloat16)
 
 
-def prepare_kernel(x_ref, m_ref, o_ref, p_ref):
+def prepare_kernel(x_hbm, m_hbm, o_hbm, p_ref, x_ref, m_ref, o_ref, sems):
+    load_m = pltpu.make_async_copy(m_hbm, m_ref, sems.at[0])
+    load_m.start()
+    load_x = pltpu.make_async_copy(x_hbm, x_ref, sems.at[1])
+    load_x.start()
+    load_m.wait()
     pack_matrix(m_ref, p_ref)
-    x = x_ref[...].astype(jnp.float32)
-    sides = []
-    for c in range(2):
-        rows = jnp.concatenate(
-            [x[0, :, c, :], x[1, :, c, :], jnp.zeros((4, 768), jnp.float32)], axis=0
+    load_x.wait()
+    leaving = []
+    for h in range(2):
+        sides = []
+        for c in range(2):
+            x = x_ref[:, :, :, h * 384 : h * 384 + 384].astype(jnp.float32)
+            rows = jnp.concatenate(
+                [x[0, :, c, :], x[1, :, c, :], jnp.zeros((4, 384), jnp.float32)], axis=0
+            )
+            sides.append(rows.T[:, 0:68])
+        both = jnp.stack(sides, axis=1).astype(jnp.bfloat16).reshape(2, 2, 6, 2, 4, 2, 2, 68)
+        for l in range(2):
+            for yh in range(2):
+                for zh in range(6):
+                    for zl in range(2):
+                        o_ref[yh, zl, :, 2 * h + l, zh] = both[l, yh, zh, zl]
+        part = pl.ds(2 * h, 2)
+        leave = pltpu.make_async_copy(
+            o_ref.at[:, :, :, part], o_hbm.at[:, :, :, part], sems.at[2 + h]
         )
-        sides.append(rows.T[:, 0:68])
-    both = jnp.stack(sides, axis=1).astype(jnp.bfloat16).reshape(4, 2, 12, 8, 2, 68)
-    for l in range(4):
-        for yh in range(2):
-            for z in range(12):
-                o_ref[yh, :, l, z] = both[l, yh, z]
-
-
-def solve_kernel(x_ref, m_ref, c_ref, o_ref, stage, sol):
+        leave.start()
+        leaving.append(leave)
+    for leave in leaving:
+        leave.wait()
+
+
+def solve_kernel(x_ref, m_ref, c_ref, o_hbm, stage, sol, o_ref, sems):
     nz = m_ref.shape[0]
     for l in range(4):
         for c in range(2):
@@ -97,26 +115,41 @@
                     ],
                     axis=1,
                 )
+    leaving = []
     for l in range(4):
         o_ref[:, l] = jnp.stack([stage[l, 0], stage[l, 1]], axis=1).astype(jnp.bfloat16)
-
-
-def finish_kernel(m_ref, b_ref, heat_ref, div_ref, temp_ref, stage):
+        leave = pltpu.make_async_copy(o_ref.at[:, l], o_hbm.at[:, l], sems.at[l])
+        leave.start()
+        leaving.append(leave)
+    for leave in leaving:
+        leave.wait()
+
+
+def place_kernel(q_ref):
+    for g in range(3):
+        row = lax.broadcasted_iota(jnp.int32, (256, 768), 0)
+        col = lax.broadcasted_iota(jnp.int32, (256, 768), 1)
+        q, s, l = 4 * g + (row >> 6), (row >> 2) & 15, row & 3
+        yh, zl, x = s >> 3, (s >> 2) & 1, s & 3
+        place = l * 192 + yh * 96 + (q >> 1) * 16 + zl * 8 + x * 2 + (q & 1)
+        q_ref[g * 256 : g * 256 + 256, :] = jnp.where(col == place, 1.0, 0.0).astype(
+            jnp.bfloat16
+        )
+
+
+def finish_kernel(
+    m_ref, b_ref, heat_ref, q_ref, div_hbm, temp_hbm, stage, div_ref, temp_ref, sems
+):
     full = b_ref[...].astype(jnp.float32)
     spans = []
     for c in range(2):
         flipped = full[:, c, :].T
-        spans.append([flipped[z * 136 : (z + 1) * 136, :] for z in range(12)])
+        spans.append([flipped[q * 136 : (q + 1) * 136, :] for q in range(12)])
     total = None
     for g in range(3):
         sides = [jnp.concatenate(spans[c][4 * g : 4 * g + 4], axis=1) for c in range(2)]
         left = jnp.concatenate(sides, axis=0).astype(jnp.bfloat16)
-        row = lax.broadcasted_iota(jnp.int32, (256, 768), 0)
-        col = lax.broadcasted_iota(jnp.int32, (256, 768), 1)
-        z, s, l = 4 * g + (row >> 6), (row >> 2) & 15, row & 3
-        place = l * 192 + (s >> 3) * 96 + z * 8 + (s & 7)
-        put = jnp.where(col == place, 1.0, 0.0).astype(jnp.bfloat16)
-        part = dot(left, put, NN)
+        part = dot(left, q_ref[g * 256 : g * 256 + 256, :], NN)
         total = part if total is None else total + part
     for c in range(2):
         for t in range(6):
@@ -124,6 +157,7 @@
                 c * 136 : (c + 1) * 136, t * 128 : (t + 1) * 128
             ]
     lane = lax.broadcasted_iota(jnp.int32, (2, 768), 1)
+    leaving = []
     for r in range(2):
         inside = lane >= m_ref[r]
         for k in range(34):
@@ -135,10 +169,21 @@
             heat = heat_ref[r, k].astype(jnp.float32)
             div_ref[r, k] = jnp.where(inside, solved, 0.0).astype(jnp.bfloat16)
             temp_ref[r, k] = jnp.where(inside, heat - coupled, 0.0).astype(jnp.bfloat16)
-
-
-def vmem(n):
-    return [pl.BlockSpec(memory_space=pltpu.VMEM)] * n
+        for f, (ready, out) in enumerate(((div_ref, div_hbm), (temp_ref, temp_hbm))):
+            leave = pltpu.make_async_copy(ready.at[r], out.at[r], sems.at[2 * r + f])
+            leave.start()
+            leaving.append(leave)
+    for leave in leaving:
+        leave.wait()
+
+
+VMEM = pl.BlockSpec(memory_space=pltpu.VMEM)
+SMEM = pl.BlockSpec(memory_space=pltpu.SMEM)
+HBM = pl.BlockSpec(memory_space=pltpu.HBM)
+
+
+def copies(n):
+    return pltpu.SemaphoreType.DMA((n,))
 
 
 def on_device(
@@ -151,54 +196,78 @@
     azimuthal_order_list,
 ):
     rows, parts, lev_local, total_n = spreading_source.shape
-    nyh, nz, nx, nc = (lax.axis_size(a) for a in WAVE)
+    nyh, nzh, nzl, nx, nc = (lax.axis_size(a) for a in WAVE)
     nlev = lax.axis_size("lev")
-    peers = nyh * nx * nc
+    peers = nyh * nzl * nx
+    shared = nzh * nc
     layers = lev_local * nlev
     zero = jnp.zeros((), jnp.bfloat16)
 
+    def bf16(*shape):
+        return jax.ShapeDtypeStruct(shape, jnp.bfloat16)
+
+    def room(*shape, dtype=jnp.bfloat16):
+        return pltpu.VMEM(shape, dtype)
+
+    outgoing = (nyh, nzl, nx, nlev, nzh, nc, parts, rows * lev_local)
     sent, packed = pl.pallas_call(
         prepare_kernel,
-        out_shape=(
-            jax.ShapeDtypeStruct((nyh, nx * nc, nlev, nz, parts, rows * lev_local), jnp.bfloat16),
-            jax.ShapeDtypeStruct((layers + 16, 128), jnp.bfloat16),
-        ),
-        in_specs=vmem(2),
-        out_specs=tuple(vmem(2)),
+        out_shape=(bf16(*outgoing), bf16(layers + 16, 128)),
+        in_specs=[HBM, HBM],
+        out_specs=(HBM, VMEM),
+        scratch_shapes=[
+            room(rows, lev_local, parts, total_n),
+            room(layers, layers),
+            room(*outgoing),
+            copies(4),
+        ],
         compiler_params=LIMIT,
-    )(spreading_source.transpose(0, 2, 1, 3), helmholtz_inverses[0, 0])
-    sent = sent.reshape(peers * nlev, nz, parts, rows * lev_local)
+    )(
+        pltpu.with_memory_space_constraint(spreading_source.transpose(0, 2, 1, 3), pltpu.HBM),
+        pltpu.with_memory_space_constraint(helmholtz_inverses[0, 0], pltpu.HBM),
+    )
+    sent = sent.reshape(peers * nlev, shared, parts, rows * lev_local)
     got = lax.all_to_all(sent, PEERS, split_axis=0, concat_axis=0, tiled=True)
-    matrices = lax.all_gather(packed, "z", axis=0, tiled=False)
+    matrices = lax.all_gather(packed, SHARERS, axis=0, tiled=False)
 
     width = 13 * 128
     both = pl.pallas_call(
         solve_kernel,
-        out_shape=jax.ShapeDtypeStruct((peers, nlev, parts, width), jnp.bfloat16),
-        in_specs=vmem(3),
-        out_specs=vmem(1)[0],
+        out_shape=bf16(peers, nlev, parts, width),
+        in_specs=[VMEM] * 3,
+        out_specs=HBM,
         scratch_shapes=[
-            pltpu.VMEM((nlev, parts, peers, width), jnp.float32),
-            pltpu.VMEM((nz * parts * rows * peers, layers), jnp.bfloat16),
+            room(nlev, parts, peers, width, dtype=jnp.float32),
+            room(shared * parts * rows * peers, layers),
+            room(peers, nlev, parts, width),
+            copies(4),
         ],
         compiler_params=LIMIT,
     )(
-        got.reshape(peers, nlev, nz, parts, rows * lev_local),
+        got.reshape(peers, nlev, shared, parts, rows * lev_local),
         matrices,
         heat_spreading_coupler,
     )
     both = both.reshape(peers * nlev, parts, width)
     back = lax.all_to_all(both, PEERS, split_axis=0, concat_axis=0, tiled=True)
 
-    out = jax.ShapeDtypeStruct((rows, lev_local, parts, total_n), jnp.bfloat16)
+    places = pl.pallas_call(
+        place_kernel, out_shape=bf16(total_n, total_n), out_specs=VMEM, compiler_params=LIMIT
+    )()
+    spectrum = (rows, lev_local, parts, total_n)
     divergence, temperature = pl.pallas_call(
         finish_kernel,
-        out_shape=(out, out),
-        in_specs=[pl.BlockSpec(memory_space=pltpu.SMEM)] + vmem(2),
-        out_specs=tuple(vmem(2)),
-        scratch_shapes=[pltpu.VMEM((total_n // 128, 4 * rows * lev_local, 128), jnp.float32)],
+        out_shape=(bf16(*spectrum), bf16(*spectrum)),
+        in_specs=[SMEM] + [VMEM] * 3,
+        out_specs=(HBM, HBM),
+        scratch_shapes=[
+            room(total_n // 128, 4 * rows * lev_local, 128, dtype=jnp.float32),
+            room(*spectrum),
+            room(*spectrum),
+            copies(4),
+        ],
         compiler_params=LIMIT,
-    )(azimuthal_order_list, back, heat_source.transpose(0, 2, 1, 3))
+    )(azimuthal_order_list, back, heat_source.transpose(0, 2, 1, 3), places)
 
     level_gain = lax.dynamic_slice_in_dim(
         smoothing_strengths, lax.axis_index("lev") * lev_local, lev_local

time: 83.1 us -> 74.4 us (0.90)
  starting transfers between devices: 29.5 us -> 23 us
  local copies, waits for them, and re-layouts: 3.22 us -> 0.11 us
  Pallas kernels: 7.63 us -> 8.8 us
    all_to_all x1, starting transfers between devices: 14.9 us -> 10.1 us  [on_device(): back = lax.all_to_all(both, PEERS, split_axis=0, concat_axis=0, tiled=True)]
    unnamed x14 -> x10, local copies, waits for them, and re-layouts: 3.14 us -> 0.03 us
    all_to_all x1, starting transfers between devices: 14.6 us -> 12.9 us  [on_device(): got = lax.all_to_all(sent, PEERS, split_axis=0, concat_axis=0, tiled=True)]
    pallas_call x3 -> x4, Pallas kernels: 7.63 us -> 8.8 us  [the longest x1 3.14 us: on_device(): pl.pallas_call(solve_kernel, out_shape=bf16(peers, nlev, parts, width), i...]
  transfers between devices with their start and end apart: 2 -> 2, of which waited for: 1 -> 1; matrix products, arithmetic and copies ran while one was open for 1% -> 2% of each run, Pallas kernels for 0% -> 1%
where the time goes in v4:
time: 74.4 us; the launch traced here: 73.8 us
  blocking collectives  27.8 us (37%)
  starting transfers between devices  23 us (31%)
  waiting for transfers between devices  12.2 us (16%)
  Pallas kernels  8.8 us (12%)
  other arithmetic  1.08 us (1%)
    all_gather x1, blocking collectives, on_device(): matrices = lax.all_gather(packed, SHARERS, axis=0, tiled=False)  27.8 us
    all_to_all x1, starting transfers between devices, on_device(): got = lax.all_to_all(sent, PEERS, split_axis=0, concat_axis=0, tiled=True)  12.9 us
    all_to_all x1, waiting for transfers between devices, on_device(): back = lax.all_to_all(both, PEERS, split_axis=0, concat_axis=0, tiled=True)  12.2 us
    all_to_all x1, starting transfers between devices, on_device(): back = lax.all_to_all(both, PEERS, split_axis=0, concat_axis=0, tiled=True)  10.1 us
    pallas_call x1, Pallas kernels, on_device(): pl.pallas_call(solve_kernel, out_shape=bf16(peers, nlev, parts, width), i...  3.14 us
    pallas_call x1, Pallas kernels, on_device(): pl.pallas_call(finish_kernel, out_shape=(bf16(*spectrum), bf16(*spectrum)...  2.64 us
    pallas_call x1, Pallas kernels, on_device(): pl.pallas_call(prepare_kernel, out_shape=(bf16(*outgoing), bf16(layers +...  2.6 us
  transfers between devices with their start and end apart: 2, of which 1 were waited for; matrix products, arithmetic and copies ran while one was open for 2% of the time, Pallas kernels for 1%

profile of v4, /device:TPU:1, one launch (start us, length us, event | category | flops | bytes accessed | tf_op | source)
XLA Modules:
  0.0 73.8 jit_solution(5068090958666154252)
XLA Ops:
  0.6 0.0 copy-start.1
  0.6 2.6 %shard_map.94 = (bf16[2,2,4,4,6,2,2,68]{7,6,5,4,3,2,1,0:T(2,128)(2,1)}, bf16[152,128]{1,0:T(8,128)(2,1)S(1)}) custom-call(bf16[2,34,2,768]{3,2,1,0:T(2,128)(2,1)} %bitcast.12, bf16[136,136]{1,0:T(8,128)(2,1)} %bitcast.13), custom_call_target="tpu_custom_call" | custom-call | tf_op jit(solution)/shard_map/pallas_call | solution.py:213
  3.2 12.9 %all-to-all-start = ((bf16[64,12,2,68]{3,2,1,0:T(2,128)(2,1)}), bf16[64,12,2,68]{3,2,1,0:T(2,128)(2,1)S(1)}, u32[]{:S(2)}, u32[]{:S(2)}) async-start(bf16[64,12,2,68]{3,2,1,0:T(2,128)(2,1)} %bitcast.2), calls=%async_computation | async-start | bytes 786432 | tf_op jit(solution)/shard_map/all_to_all | solution.py:230
  16.2 27.8 %all-gather = bf16[1824,128]{1,0:T(8,128)(2,1)S(1)} all-gather(bf16[152,128]{1,0:T(8,128)(2,1)S(1)} %get-tuple-element.8), channel_id=2, replica_groups=mesh['yh'=2,'zh'=6,'zl'=2,'x'=4,'c'=2,'lev'=4] {'zh','c'}, dimensions={0}, use_global_device_ids=true | all-gather | bytes 505856 | tf_op jit(solution)/shard_map/all_gather | solution.py:231
  44.0 0.0 all-to-all-done
  44.0 0.0 copy-done.1
  44.0 3.1 %shard_map.95 = bf16[16,4,2,1664]{3,2,1,0:T(2,128)(2,1)} custom-call(bf16[16,4,12,2,68]{4,3,2,1,0:T(2,128)(2,1)S(1)} %bitcast.10, bf16[12,152,128]{2,1,0:T(8,128)(2,1)S(1)} %bitcast.9, bf16[136,136]{1,0:T(8,128)(2,1)S(1)} %copy-done.1), custom_call_target="tpu_custom_call" | custom-call | tf_op jit(solution)/shard_map/pallas_call | solution.py:234
  47.2 0.0 copy-start.4
  47.2 0.0 copy-start.2
  47.2 0.0 copy-start.3
  47.2 0.0 copy-start
  47.2 10.1 %all-to-all-start.1 = ((bf16[64,2,1664]{2,1,0:T(2,128)(2,1)}), bf16[64,2,1664]{2,1,0:T(2,128)(2,1)S(1)}, u32[]{:S(2)}, u32[]{:S(2)}) async-start(bf16[64,2,1664]{2,1,0:T(2,128)(2,1)} %bitcast.5), calls=%async_computation.1 | async-start | bytes 851968 | tf_op jit(solution)/shard_map/all_to_all | solution.py:252
  57.3 0.4 shard_map.96.q_ref
  57.8 0.0 copy-done.4
  57.8 0.1 dynamic_slice.3
  57.9 0.0 copy-done.2
  57.9 0.1 iota_compare_fusion
  57.9 0.1 add_divide_fusion
  58.0 0.0 copy-done.3
  58.0 0.9 %broadcast_select_fusion = bf16[2,2,34,768]{3,1,2,0:T(2,128)(2,1)} fusion(pred[2,768]{1,0:T(4,128)(4,1)S(1)} %iota_compare_fusion, bf16[2,2,34,768]{3,1,2,0:T(2,128)(2,1)S(1)} %copy-done.3, f32[34,768]{1,0:T(8,128)S(1)} %add_divide_fusion), kind=kLoop, calls=%fused_computation.1 | loop fusion | flops 417792 | bytes 523776 | tf_op jit(solution)/shard_map/jit(_where)/select_n | solution.py:281
  59.0 12.2 %all-to-all-done.1.b_ref = bf16[64,2,1664]{2,1,0:T(2,128)(2,1)S(1)} async-done(((bf16[64,2,1664]{2,1,0:T(2,128)(2,1)}), bf16[64,2,1664]{2,1,0:T(2,128)(2,1)S(1)}, u32[]{:S(2)}, u32[]{:S(2)}) %all-to-all-start.1) | async-done | bytes 426016 | tf_op jit(solution)/shard_map/all_to_all | solution.py:252
  71.1 0.0 copy-done
  71.1 2.6 %shard_map.97 = (bf16[2,34,2,768]{3,2,1,0:T(2,128)(2,1)}, bf16[2,34,2,768]{3,2,1,0:T(2,128)(2,1)}) custom-call(s32[2]{0:T(128)S(1)} %copy-done.2, bf16[64,2,1664]{2,1,0:T(2,128)(2,1)S(1)} %all-to-all-done.1.b_ref, bf16[2,34,2,768]{3,2,1,0:T(2,128)(2,1)S(1)} %bitcast.11, bf16[768,768]{1,0:T(8,128)(2,1)S(1)} %shard_map.96.q_ref), custom_call_target="tpu_custom_call" | custom-call | tf_op jit(solution)/shard_map/pallas_call | solution.py:258
  (1 shorter events, 0.0 us)
Async XLA Ops:
  0.6 43.4 %copy-start.1 = (bf16[136,136]{1,0:T(8,128)(2,1)S(1)}, bf16[136,136]{1,0:T(8,128)(2,1)}, u32[]{:S(2)}) copy-start(bf16[136,136]{1,0:T(8,128)(2,1)} %c_ref.1) | copy-start | bytes 110980
  3.2 40.8 %all-to-all-start = ((bf16[64,12,2,68]{3,2,1,0:T(2,128)(2,1)}), bf16[64,12,2,68]{3,2,1,0:T(2,128)(2,1)S(1)}, u32[]{:S(2)}, u32[]{:S(2)}) async-start(bf16[64,12,2,68]{3,2,1,0:T(2,128)(2,1)} %bitcast.2), calls=%async_computation | async-start | bytes 786432 | tf_op jit(solution)/shard_map/all_to_all | solution.py:230
  47.2 10.6 %copy-start.4 = (f32[136]{0:T(256)S(1)}, f32[136]{0:T(256)}, u32[]{:S(2)}) copy-start(f32[136]{0:T(256)} %param.12) | copy-start | bytes 1636
  47.2 10.7 %copy-start.2 = (s32[2]{0:T(128)S(1)}, s32[2]{0:T(128)}, u32[]{:S(2)}) copy-start(s32[2]{0:T(128)} %m_ref.1) | copy-start | bytes 28
  47.2 10.8 %copy-start.3 = (bf16[2,2,34,768]{3,1,2,0:T(2,128)(2,1)S(1)}, bf16[2,2,34,768]{3,1,2,0:T(2,128)(2,1)}, u32[]{:S(2)}) copy-start(bf16[2,2,34,768]{3,1,2,0:T(2,128)(2,1)} %param.7) | copy-start | bytes 626692
  47.2 23.9 %copy-start = (bf16[2,2,34,768]{3,1,2,0:T(2,128)(2,1)S(1)}, bf16[2,2,34,768]{3,1,2,0:T(2,128)(2,1)}, u32[]{:S(2)}) copy-start(bf16[2,2,34,768]{3,1,2,0:T(2,128)(2,1)} %param.9) | copy-start | bytes 626692
  47.2 23.9 %all-to-all-start.1 = ((bf16[64,2,1664]{2,1,0:T(2,128)(2,1)}), bf16[64,2,1664]{2,1,0:T(2,128)(2,1)S(1)}, u32[]{:S(2)}, u32[]{:S(2)}) async-start(bf16[64,2,1664]{2,1,0:T(2,128)(2,1)} %bitcast.5), calls=%async_computation.1 | async-start | bytes 851968 | tf_op jit(solution)/shard_map/all_to_all | solution.py:252

commit v5 on v4

--- a/solution.py
+++ b/solution.py
@@ -72,17 +72,14 @@
         leave.wait()
 
 
-def solve_kernel(x_ref, m_ref, c_ref, o_hbm, stage, sol, o_ref, sems):
+def solve_kernel(x_ref, m_ref, c_ref, o_hbm, stage, sol, o_ref, pairs, sems):
     nz = m_ref.shape[0]
-    for l in range(4):
-        for c in range(2):
-            stage[l, c, :, 1536:1664] = jnp.zeros((16, 128), jnp.float32)
     for z in range(nz):
         parts = ([], [])
         for l in range(4):
-            got = x_ref[:, l, z].astype(jnp.float32)
+            pairs[z * 4 + l, :, 0:68] = x_ref[:, l, z].reshape(32, 68).astype(jnp.float32)
             for c in range(2):
-                parts[c].append(got[:, c, :])
+                parts[c].append(pairs[z * 4 + l, pl.ds(c, 16, 2), :])
         x = jnp.concatenate(
             [
                 jnp.concatenate(
@@ -117,7 +114,17 @@
                 )
     leaving = []
     for l in range(4):
-        o_ref[:, l] = jnp.stack([stage[l, 0], stage[l, 1]], axis=1).astype(jnp.bfloat16)
+        for t in range(13):
+            for c in range(2):
+                tile = stage[l, c, :, t * 128 : t * 128 + 128]
+                if t == 12:
+                    tile = jnp.concatenate(
+                        [tile[:, 0:96], jnp.zeros((16, 32), jnp.float32)], axis=1
+                    )
+                pairs[l * 13 + t, pl.ds(c, 16, 2), :] = tile
+            o_ref[:, l, :, t * 128 : t * 128 + 128] = (
+                pairs[l * 13 + t].astype(jnp.bfloat16).reshape(16, 2, 128)
+            )
         leave = pltpu.make_async_copy(o_ref.at[:, l], o_hbm.at[:, l], sems.at[l])
         leave.start()
         leaving.append(leave)
@@ -240,6 +247,7 @@
             room(nlev, parts, peers, width, dtype=jnp.float32),
             room(shared * parts * rows * peers, layers),
             room(peers, nlev, parts, width),
+            room(nlev * 13, parts * peers, 128, dtype=jnp.float32),
             copies(4),
         ],
         compiler_params=LIMIT,

time: 74.4 us -> 73.7 us (level)
  no operation moved by 1% of the time
where the time goes in v5:
time: 73.7 us; the launch traced here: 73 us
  blocking collectives  27.8 us (38%)
  starting transfers between devices  23 us (31%)
  waiting for transfers between devices  12.2 us (17%)
  Pallas kernels  8.08 us (11%)
  other arithmetic  1.08 us (1%)
  between operations  0.74 us (1%)
    all_gather x1, blocking collectives, on_device(): matrices = lax.all_gather(packed, SHARERS, axis=0, tiled=False)  27.8 us
    all_to_all x1, starting transfers between devices, on_device(): got = lax.all_to_all(sent, PEERS, split_axis=0, concat_axis=0, tiled=True)  12.9 us
    all_to_all x1, waiting for transfers between devices, on_device(): back = lax.all_to_all(both, PEERS, split_axis=0, concat_axis=0, tiled=True)  12.2 us
    all_to_all x1, starting transfers between devices, on_device(): back = lax.all_to_all(both, PEERS, split_axis=0, concat_axis=0, tiled=True)  10.1 us
    pallas_call x1, Pallas kernels, on_device(): pl.pallas_call(finish_kernel, out_shape=(bf16(*spectrum), bf16(*spectrum)...  2.64 us
    pallas_call x1, Pallas kernels, on_device(): pl.pallas_call(prepare_kernel, out_shape=(bf16(*outgoing), bf16(layers +...  2.6 us
    pallas_call x1, Pallas kernels, on_device(): pl.pallas_call(solve_kernel, out_shape=bf16(peers, nlev, parts, width), i...  2.42 us
  transfers between devices with their start and end apart: 2, of which 1 were waited for; matrix products, arithmetic and copies ran while one was open for 2% of the time, Pallas kernels for 1%

profile of v5, /device:TPU:1, one launch (start us, length us, event | category | flops | bytes accessed | tf_op | source)
XLA Modules:
  0.0 73.0 jit_solution(6441263712280308639)
XLA Ops:
  0.6 0.0 copy-start.1
  0.6 2.6 %shard_map.94 = (bf16[2,2,4,4,6,2,2,68]{7,6,5,4,3,2,1,0:T(2,128)(2,1)}, bf16[152,128]{1,0:T(8,128)(2,1)S(1)}) custom-call(bf16[2,34,2,768]{3,2,1,0:T(2,128)(2,1)} %bitcast.12, bf16[136,136]{1,0:T(8,128)(2,1)} %bitcast.13), custom_call_target="tpu_custom_call" | custom-call | tf_op jit(solution)/shard_map/pallas_call | solution.py:220
  3.2 12.9 %all-to-all-start = ((bf16[64,12,2,68]{3,2,1,0:T(2,128)(2,1)}), bf16[64,12,2,68]{3,2,1,0:T(2,128)(2,1)S(1)}, u32[]{:S(2)}, u32[]{:S(2)}) async-start(bf16[64,12,2,68]{3,2,1,0:T(2,128)(2,1)} %bitcast.2), calls=%async_computation | async-start | bytes 786432 | tf_op jit(solution)/shard_map/all_to_all | solution.py:237
  16.2 27.8 %all-gather = bf16[1824,128]{1,0:T(8,128)(2,1)S(1)} all-gather(bf16[152,128]{1,0:T(8,128)(2,1)S(1)} %get-tuple-element.8), channel_id=2, replica_groups=mesh['yh'=2,'zh'=6,'zl'=2,'x'=4,'c'=2,'lev'=4] {'zh','c'}, dimensions={0}, use_global_device_ids=true | all-gather | bytes 505856 | tf_op jit(solution)/shard_map/all_gather | solution.py:238
  44.0 0.0 all-to-all-done
  44.0 0.0 copy-done.1
  44.0 2.4 %shard_map.95 = bf16[16,4,2,1664]{3,2,1,0:T(2,128)(2,1)} custom-call(bf16[16,4,12,2,68]{4,3,2,1,0:T(2,128)(2,1)S(1)} %bitcast.10, bf16[12,152,128]{2,1,0:T(8,128)(2,1)S(1)} %bitcast.9, bf16[136,136]{1,0:T(8,128)(2,1)S(1)} %copy-done.1), custom_call_target="tpu_custom_call" | custom-call | tf_op jit(solution)/shard_map/pallas_call | solution.py:241
  46.5 0.0 copy-start.4
  46.5 0.0 copy-start.2
  46.5 0.0 copy-start.3
  46.5 0.0 copy-start
  46.5 10.1 %all-to-all-start.1 = ((bf16[64,2,1664]{2,1,0:T(2,128)(2,1)}), bf16[64,2,1664]{2,1,0:T(2,128)(2,1)S(1)}, u32[]{:S(2)}, u32[]{:S(2)}) async-start(bf16[64,2,1664]{2,1,0:T(2,128)(2,1)} %bitcast.5), calls=%async_computation.1 | async-start | bytes 851968 | tf_op jit(solution)/shard_map/all_to_all | solution.py:260
  56.6 0.4 shard_map.96.q_ref
  57.0 0.0 copy-done.4
  57.1 0.1 dynamic_slice.3
  57.1 0.0 copy-done.2
  57.1 0.1 iota_compare_fusion
  57.2 0.1 add_divide_fusion
  57.3 0.0 copy-done.3
  57.3 0.9 %broadcast_select_fusion = bf16[2,2,34,768]{3,1,2,0:T(2,128)(2,1)} fusion(pred[2,768]{1,0:T(4,128)(4,1)S(1)} %iota_compare_fusion, bf16[2,2,34,768]{3,1,2,0:T(2,128)(2,1)S(1)} %copy-done.3, f32[34,768]{1,0:T(8,128)S(1)} %add_divide_fusion), kind=kLoop, calls=%fused_computation.1 | loop fusion | flops 417792 | bytes 523776 | tf_op jit(solution)/shard_map/jit(_where)/select_n | solution.py:289
  58.2 12.2 %all-to-all-done.1.b_ref = bf16[64,2,1664]{2,1,0:T(2,128)(2,1)S(1)} async-done(((bf16[64,2,1664]{2,1,0:T(2,128)(2,1)}), bf16[64,2,1664]{2,1,0:T(2,128)(2,1)S(1)}, u32[]{:S(2)}, u32[]{:S(2)}) %all-to-all-start.1) | async-done | bytes 426016 | tf_op jit(solution)/shard_map/all_to_all | solution.py:260
  70.4 0.0 copy-done
  70.4 2.6 %shard_map.97 = (bf16[2,34,2,768]{3,2,1,0:T(2,128)(2,1)}, bf16[2,34,2,768]{3,2,1,0:T(2,128)(2,1)}) custom-call(s32[2]{0:T(128)S(1)} %copy-done.2, bf16[64,2,1664]{2,1,0:T(2,128)(2,1)S(1)} %all-to-all-done.1.b_ref, bf16[2,34,2,768]{3,2,1,0:T(2,128)(2,1)S(1)} %bitcast.11, bf16[768,768]{1,0:T(8,128)(2,1)S(1)} %shard_map.96.q_ref), custom_call_target="tpu_custom_call" | custom-call | tf_op jit(solution)/shard_map/pallas_call | solution.py:266
  (1 shorter events, 0.0 us)
Async XLA Ops:
  0.6 43.4 %copy-start.1 = (bf16[136,136]{1,0:T(8,128)(2,1)S(1)}, bf16[136,136]{1,0:T(8,128)(2,1)}, u32[]{:S(2)}) copy-start(bf16[136,136]{1,0:T(8,128)(2,1)} %c_ref.1) | copy-start | bytes 110980
  3.2 40.8 %all-to-all-start = ((bf16[64,12,2,68]{3,2,1,0:T(2,128)(2,1)}), bf16[64,12,2,68]{3,2,1,0:T(2,128)(2,1)S(1)}, u32[]{:S(2)}, u32[]{:S(2)}) async-start(bf16[64,12,2,68]{3,2,1,0:T(2,128)(2,1)} %bitcast.2), calls=%async_computation | async-start | bytes 786432 | tf_op jit(solution)/shard_map/all_to_all | solution.py:237
  46.5 10.6 %copy-start.4 = (f32[136]{0:T(256)S(1)}, f32[136]{0:T(256)}, u32[]{:S(2)}) copy-start(f32[136]{0:T(256)} %param.12) | copy-start | bytes 1636
  46.5 10.7 %copy-start.2 = (s32[2]{0:T(128)S(1)}, s32[2]{0:T(128)}, u32[]{:S(2)}) copy-start(s32[2]{0:T(128)} %m_ref.1) | copy-start | bytes 28
  46.5 10.8 %copy-start.3 = (bf16[2,2,34,768]{3,1,2,0:T(2,128)(2,1)S(1)}, bf16[2,2,34,768]{3,1,2,0:T(2,128)(2,1)}, u32[]{:S(2)}) copy-start(bf16[2,2,34,768]{3,1,2,0:T(2,128)(2,1)} %param.7) | copy-start | bytes 626692
  46.5 23.9 %copy-start = (bf16[2,2,34,768]{3,1,2,0:T(2,128)(2,1)S(1)}, bf16[2,2,34,768]{3,1,2,0:T(2,128)(2,1)}, u32[]{:S(2)}) copy-start(bf16[2,2,34,768]{3,1,2,0:T(2,128)(2,1)} %param.9) | copy-start | bytes 626692
  46.5 23.9 %all-to-all-start.1 = ((bf16[64,2,1664]{2,1,0:T(2,128)(2,1)}), bf16[64,2,1664]{2,1,0:T(2,128)(2,1)S(1)}, u32[]{:S(2)}, u32[]{:S(2)}) async-start(bf16[64,2,1664]{2,1,0:T(2,128)(2,1)} %bitcast.5), calls=%async_computation.1 | async-start | bytes 851968 | tf_op jit(solution)/shard_map/all_to_all | solution.py:260

commit v6 on v5

--- a/solution.py
+++ b/solution.py
@@ -6,7 +6,7 @@
 from jax.sharding import Mesh, PartitionSpec as P
 
 WAVE = ("yh", "zh", "zl", "x", "c")
-PEERS = ("yh", "zl", "x", "lev")
+PEERS = ("lev", "x", "zl", "yh")
 SHARERS = ("zh", "c")
 NT = (((1,), (1,)), ((), ()))
 NN = (((1,), (0,)), ((), ()))
@@ -61,10 +61,10 @@
             for yh in range(2):
                 for zh in range(6):
                     for zl in range(2):
-                        o_ref[yh, zl, :, 2 * h + l, zh] = both[l, yh, zh, zl]
+                        o_ref[2 * h + l, :, zl, yh, zh] = both[l, yh, zh, zl]
         part = pl.ds(2 * h, 2)
         leave = pltpu.make_async_copy(
-            o_ref.at[:, :, :, part], o_hbm.at[:, :, :, part], sems.at[2 + h]
+            o_ref.at[part], o_hbm.at[part], sems.at[2 + h]
         )
         leave.start()
         leaving.append(leave)
@@ -77,7 +77,7 @@
     for z in range(nz):
         parts = ([], [])
         for l in range(4):
-            pairs[z * 4 + l, :, 0:68] = x_ref[:, l, z].reshape(32, 68).astype(jnp.float32)
+            pairs[z * 4 + l, :, 0:68] = x_ref[l, :, z].reshape(32, 68).astype(jnp.float32)
             for c in range(2):
                 parts[c].append(pairs[z * 4 + l, pl.ds(c, 16, 2), :])
         x = jnp.concatenate(
@@ -122,10 +122,10 @@
                         [tile[:, 0:96], jnp.zeros((16, 32), jnp.float32)], axis=1
                     )
                 pairs[l * 13 + t, pl.ds(c, 16, 2), :] = tile
-            o_ref[:, l, :, t * 128 : t * 128 + 128] = (
+            o_ref[l, :, :, t * 128 : t * 128 + 128] = (
                 pairs[l * 13 + t].astype(jnp.bfloat16).reshape(16, 2, 128)
             )
-        leave = pltpu.make_async_copy(o_ref.at[:, l], o_hbm.at[:, l], sems.at[l])
+        leave = pltpu.make_async_copy(o_ref.at[l], o_hbm.at[l], sems.at[l])
         leave.start()
         leaving.append(leave)
     for leave in leaving:
@@ -136,8 +136,8 @@
     for g in range(3):
         row = lax.broadcasted_iota(jnp.int32, (256, 768), 0)
         col = lax.broadcasted_iota(jnp.int32, (256, 768), 1)
-        q, s, l = 4 * g + (row >> 6), (row >> 2) & 15, row & 3
-        yh, zl, x = s >> 3, (s >> 2) & 1, s & 3
+        q, l = 4 * g + (row >> 6), (row >> 4) & 3
+        x, zl, yh = (row >> 2) & 3, (row >> 1) & 1, row & 1
         place = l * 192 + yh * 96 + (q >> 1) * 16 + zl * 8 + x * 2 + (q & 1)
         q_ref[g * 256 : g * 256 + 256, :] = jnp.where(col == place, 1.0, 0.0).astype(
             jnp.bfloat16
@@ -216,7 +216,7 @@
     def room(*shape, dtype=jnp.bfloat16):
         return pltpu.VMEM(shape, dtype)
 
-    outgoing = (nyh, nzl, nx, nlev, nzh, nc, parts, rows * lev_local)
+    outgoing = (nlev, nx, nzl, nyh, nzh, nc, parts, rows * lev_local)
     sent, packed = pl.pallas_call(
         prepare_kernel,
         out_shape=(bf16(*outgoing), bf16(layers + 16, 128)),
@@ -240,19 +240,19 @@
     width = 13 * 128
     both = pl.pallas_call(
         solve_kernel,
-        out_shape=bf16(peers, nlev, parts, width),
+        out_shape=bf16(nlev, peers, parts, width),
         in_specs=[VMEM] * 3,
         out_specs=HBM,
         scratch_shapes=[
             room(nlev, parts, peers, width, dtype=jnp.float32),
             room(shared * parts * rows * peers, layers),
-            room(peers, nlev, parts, width),
+            room(nlev, peers, parts, width),
             room(nlev * 13, parts * peers, 128, dtype=jnp.float32),
             copies(4),
         ],
         compiler_params=LIMIT,
     )(
-        got.reshape(peers, nlev, shared, parts, rows * lev_local),
+        got.reshape(nlev, peers, shared, parts, rows * lev_local),
         matrices,
         heat_spreading_coupler,
     )

time: 73.7 us -> 74.4 us (level)
  waiting for transfers between devices: 12.2 us -> 13.4 us
    all_to_all x1, waiting for transfers between devices: 12.2 us -> 13.4 us  [on_device(): back = lax.all_to_all(both, PEERS, split_axis=0, concat_axis=0, tiled=True)]
where the time goes in v6:
time: 74.4 us; the launch traced here: 74.1 us
  blocking collectives  27.8 us (37%)
  starting transfers between devices  22.9 us (31%)
  waiting for transfers between devices  13.4 us (18%)
  Pallas kernels  8.02 us (11%)
  other arithmetic  1.08 us (1%)
    all_gather x1, blocking collectives, on_device(): matrices = lax.all_gather(packed, SHARERS, axis=0, tiled=False)  27.8 us
    all_to_all x1, waiting for transfers between devices, on_device(): back = lax.all_to_all(both, PEERS, split_axis=0, concat_axis=0, tiled=True)  13.4 us
    all_to_all x1, starting transfers between devices, on_device(): got = lax.all_to_all(sent, PEERS, split_axis=0, concat_axis=0, tiled=True)  12.9 us
    all_to_all x1, starting transfers between devices, on_device(): back = lax.all_to_all(both, PEERS, split_axis=0, concat_axis=0, tiled=True)  9.93 us
    pallas_call x1, Pallas kernels, on_device(): pl.pallas_call(finish_kernel, out_shape=(bf16(*spectrum), bf16(*spectrum)...  2.64 us
    pallas_call x1, Pallas kernels, on_device(): pl.pallas_call(prepare_kernel, out_shape=(bf16(*outgoing), bf16(layers +...  2.56 us
    pallas_call x1, Pallas kernels, on_device(): pl.pallas_call(solve_kernel, out_shape=bf16(nlev, peers, parts, width), i...  2.42 us
  transfers between devices with their start and end apart: 2, of which 1 were waited for; matrix products, arithmetic and copies ran while one was open for 2% of the time, Pallas kernels for 1%

profile of v6, /device:TPU:1, one launch (start us, length us, event | category | flops | bytes accessed | tf_op | source)
XLA Modules:
  0.0 74.1 jit_solution(5649958184795339786)
XLA Ops:
  0.6 0.0 copy-start.1
  0.6 2.6 %shard_map.94 = (bf16[4,4,2,2,6,2,2,68]{7,6,5,4,3,2,1,0:T(2,128)(2,1)}, bf16[152,128]{1,0:T(8,128)(2,1)S(1)}) custom-call(bf16[2,34,2,768]{3,2,1,0:T(2,128)(2,1)} %bitcast.12, bf16[136,136]{1,0:T(8,128)(2,1)} %bitcast.13), custom_call_target="tpu_custom_call" | custom-call | tf_op jit(solution)/shard_map/pallas_call | solution.py:220
  3.2 12.9 %all-to-all-start = ((bf16[64,12,2,68]{3,2,1,0:T(2,128)(2,1)}), bf16[64,12,2,68]{3,2,1,0:T(2,128)(2,1)S(1)}, u32[]{:S(2)}, u32[]{:S(2)}) async-start(bf16[64,12,2,68]{3,2,1,0:T(2,128)(2,1)} %bitcast.2), calls=%async_computation | async-start | bytes 786432 | tf_op jit(solution)/shard_map/all_to_all | solution.py:237
  16.1 27.8 %all-gather = bf16[1824,128]{1,0:T(8,128)(2,1)S(1)} all-gather(bf16[152,128]{1,0:T(8,128)(2,1)S(1)} %get-tuple-element.8), channel_id=2, replica_groups=mesh['yh'=2,'zh'=6,'zl'=2,'x'=4,'c'=2,'lev'=4] {'zh','c'}, dimensions={0}, use_global_device_ids=true | all-gather | bytes 505856 | tf_op jit(solution)/shard_map/all_gather | solution.py:238
  44.0 0.0 all-to-all-done
  44.0 0.0 copy-done.1
  44.0 2.4 %shard_map.95 = bf16[4,16,2,1664]{3,2,1,0:T(2,128)(2,1)} custom-call(bf16[4,16,12,2,68]{4,3,2,1,0:T(2,128)(2,1)S(1)} %bitcast.10, bf16[12,152,128]{2,1,0:T(8,128)(2,1)S(1)} %bitcast.9, bf16[136,136]{1,0:T(8,128)(2,1)S(1)} %copy-done.1), custom_call_target="tpu_custom_call" | custom-call | tf_op jit(solution)/shard_map/pallas_call | solution.py:241
  46.4 0.0 copy-start.4
  46.4 0.0 copy-start.2
  46.4 0.0 copy-start.3
  46.4 0.0 copy-start
  46.5 9.9 %all-to-all-start.1 = ((bf16[64,2,1664]{2,1,0:T(2,128)(2,1)}), bf16[64,2,1664]{2,1,0:T(2,128)(2,1)S(1)}, u32[]{:S(2)}, u32[]{:S(2)}) async-start(bf16[64,2,1664]{2,1,0:T(2,128)(2,1)} %bitcast.5), calls=%async_computation.1 | async-start | bytes 851968 | tf_op jit(solution)/shard_map/all_to_all | solution.py:260
  56.4 0.4 shard_map.96.q_ref
  56.8 0.0 copy-done.4
  56.8 0.1 dynamic_slice.3
  56.9 0.0 copy-done.2
  56.9 0.1 iota_compare_fusion
  57.0 0.1 add_divide_fusion
  57.1 0.0 copy-done.3
  57.1 0.9 %broadcast_select_fusion = bf16[2,2,34,768]{3,1,2,0:T(2,128)(2,1)} fusion(pred[2,768]{1,0:T(4,128)(4,1)S(1)} %iota_compare_fusion, bf16[2,2,34,768]{3,1,2,0:T(2,128)(2,1)S(1)} %copy-done.3, f32[34,768]{1,0:T(8,128)S(1)} %add_divide_fusion), kind=kLoop, calls=%fused_computation.1 | loop fusion | flops 417792 | bytes 523776 | tf_op jit(solution)/shard_map/jit(_where)/select_n | solution.py:289
  58.0 13.4 %all-to-all-done.1.b_ref = bf16[64,2,1664]{2,1,0:T(2,128)(2,1)S(1)} async-done(((bf16[64,2,1664]{2,1,0:T(2,128)(2,1)}), bf16[64,2,1664]{2,1,0:T(2,128)(2,1)S(1)}, u32[]{:S(2)}, u32[]{:S(2)}) %all-to-all-start.1) | async-done | bytes 426016 | tf_op jit(solution)/shard_map/all_to_all | solution.py:260
  71.4 0.0 copy-done
  71.4 2.6 %shard_map.97 = (bf16[2,34,2,768]{3,2,1,0:T(2,128)(2,1)}, bf16[2,34,2,768]{3,2,1,0:T(2,128)(2,1)}) custom-call(s32[2]{0:T(128)S(1)} %copy-done.2, bf16[64,2,1664]{2,1,0:T(2,128)(2,1)S(1)} %all-to-all-done.1.b_ref, bf16[2,34,2,768]{3,2,1,0:T(2,128)(2,1)S(1)} %bitcast.11, bf16[768,768]{1,0:T(8,128)(2,1)S(1)} %shard_map.96.q_ref), custom_call_target="tpu_custom_call" | custom-call | tf_op jit(solution)/shard_map/pallas_call | solution.py:266
  (1 shorter events, 0.0 us)
Async XLA Ops:
  0.6 43.3 %copy-start.1 = (bf16[136,136]{1,0:T(8,128)(2,1)S(1)}, bf16[136,136]{1,0:T(8,128)(2,1)}, u32[]{:S(2)}) copy-start(bf16[136,136]{1,0:T(8,128)(2,1)} %c_ref.1) | copy-start | bytes 110980
  3.2 40.8 %all-to-all-start = ((bf16[64,12,2,68]{3,2,1,0:T(2,128)(2,1)}), bf16[64,12,2,68]{3,2,1,0:T(2,128)(2,1)S(1)}, u32[]{:S(2)}, u32[]{:S(2)}) async-start(bf16[64,12,2,68]{3,2,1,0:T(2,128)(2,1)} %bitcast.2), calls=%async_computation | async-start | bytes 786432 | tf_op jit(solution)/shard_map/all_to_all | solution.py:237
  46.4 10.4 %copy-start.4 = (f32[136]{0:T(256)S(1)}, f32[136]{0:T(256)}, u32[]{:S(2)}) copy-start(f32[136]{0:T(256)} %param.12) | copy-start | bytes 1636
  46.4 10.5 %copy-start.2 = (s32[2]{0:T(128)S(1)}, s32[2]{0:T(128)}, u32[]{:S(2)}) copy-start(s32[2]{0:T(128)} %m_ref.1) | copy-start | bytes 28
  46.4 10.7 %copy-start.3 = (bf16[2,2,34,768]{3,1,2,0:T(2,128)(2,1)S(1)}, bf16[2,2,34,768]{3,1,2,0:T(2,128)(2,1)}, u32[]{:S(2)}) copy-start(bf16[2,2,34,768]{3,1,2,0:T(2,128)(2,1)} %param.7) | copy-start | bytes 626692
  46.4 25.0 %copy-start = (bf16[2,2,34,768]{3,1,2,0:T(2,128)(2,1)S(1)}, bf16[2,2,34,768]{3,1,2,0:T(2,128)(2,1)}, u32[]{:S(2)}) copy-start(bf16[2,2,34,768]{3,1,2,0:T(2,128)(2,1)} %param.9) | copy-start | bytes 626692
  46.5 25.0 %all-to-all-start.1 = ((bf16[64,2,1664]{2,1,0:T(2,128)(2,1)}), bf16[64,2,1664]{2,1,0:T(2,128)(2,1)S(1)}, u32[]{:S(2)}, u32[]{:S(2)}) async-start(bf16[64,2,1664]{2,1,0:T(2,128)(2,1)} %bitcast.5), calls=%async_computation.1 | async-start | bytes 851968 | tf_op jit(solution)/shard_map/all_to_all | solution.py:260

commit v7 on v5

--- a/solution.py
+++ b/solution.py
@@ -6,7 +6,7 @@
 from jax.sharding import Mesh, PartitionSpec as P
 
 WAVE = ("yh", "zh", "zl", "x", "c")
-PEERS = ("yh", "zl", "x", "lev")
+PEERS = ("zl", "x", "yh", "lev")
 SHARERS = ("zh", "c")
 NT = (((1,), (1,)), ((), ()))
 NN = (((1,), (0,)), ((), ()))
@@ -61,7 +61,7 @@
             for yh in range(2):
                 for zh in range(6):
                     for zl in range(2):
-                        o_ref[yh, zl, :, 2 * h + l, zh] = both[l, yh, zh, zl]
+                        o_ref[zl, :, yh, 2 * h + l, zh] = both[l, yh, zh, zl]
         part = pl.ds(2 * h, 2)
         leave = pltpu.make_async_copy(
             o_ref.at[:, :, :, part], o_hbm.at[:, :, :, part], sems.at[2 + h]
@@ -137,7 +137,7 @@
         row = lax.broadcasted_iota(jnp.int32, (256, 768), 0)
         col = lax.broadcasted_iota(jnp.int32, (256, 768), 1)
         q, s, l = 4 * g + (row >> 6), (row >> 2) & 15, row & 3
-        yh, zl, x = s >> 3, (s >> 2) & 1, s & 3
+        zl, x, yh = s >> 3, (s >> 1) & 3, s & 1
         place = l * 192 + yh * 96 + (q >> 1) * 16 + zl * 8 + x * 2 + (q & 1)
         q_ref[g * 256 : g * 256 + 256, :] = jnp.where(col == place, 1.0, 0.0).astype(
             jnp.bfloat16
@@ -216,7 +216,7 @@
     def room(*shape, dtype=jnp.bfloat16):
         return pltpu.VMEM(shape, dtype)
 
-    outgoing = (nyh, nzl, nx, nlev, nzh, nc, parts, rows * lev_local)
+    outgoing = (nzl, nx, nyh, nlev, nzh, nc, parts, rows * lev_local)
     sent, packed = pl.pallas_call(
         prepare_kernel,
         out_shape=(bf16(*outgoing), bf16(layers + 16, 128)),

time: 73.7 us -> 75.2 us (1.020)
  waiting for transfers between devices: 12.2 us -> 14.2 us
    all_to_all x1, waiting for transfers between devices: 12.2 us -> 14.2 us  [on_device(): back = lax.all_to_all(both, PEERS, split_axis=0, concat_axis=0, tiled=True)]
where the time goes in v7:
time: 75.2 us; the launch traced here: 74.9 us
  blocking collectives  27.9 us (37%)
  starting transfers between devices  22.8 us (30%)
  waiting for transfers between devices  14.2 us (19%)
  Pallas kernels  8.08 us (11%)
  other arithmetic  1.08 us (1%)
    all_gather x1, blocking collectives, on_device(): matrices = lax.all_gather(packed, SHARERS, axis=0, tiled=False)  27.9 us
    all_to_all x1, waiting for transfers between devices, on_device(): back = lax.all_to_all(both, PEERS, split_axis=0, concat_axis=0, tiled=True)  14.2 us
    all_to_all x1, starting transfers between devices, on_device(): got = lax.all_to_all(sent, PEERS, split_axis=0, concat_axis=0, tiled=True)  12.9 us
    all_to_all x1, starting transfers between devices, on_device(): back = lax.all_to_all(both, PEERS, split_axis=0, concat_axis=0, tiled=True)  9.89 us
    pallas_call x1, Pallas kernels, on_device(): pl.pallas_call(finish_kernel, out_shape=(bf16(*spectrum), bf16(*spectrum)...  2.64 us
    pallas_call x1, Pallas kernels, on_device(): pl.pallas_call(prepare_kernel, out_shape=(bf16(*outgoing), bf16(layers +...  2.6 us
    pallas_call x1, Pallas kernels, on_device(): pl.pallas_call(solve_kernel, out_shape=bf16(peers, nlev, parts, width), i...  2.42 us
  transfers between devices with their start and end apart: 2, of which 1 were waited for; matrix products, arithmetic and copies ran while one was open for 2% of the time, Pallas kernels for 1%

profile of v7, /device:TPU:1, one launch (start us, length us, event | category | flops | bytes accessed | tf_op | source)
XLA Modules:
  0.0 74.9 jit_solution(9308372834638820732)
XLA Ops:
  0.6 0.0 copy-start.1
  0.6 2.6 %shard_map.94 = (bf16[2,4,2,4,6,2,2,68]{7,6,5,4,3,2,1,0:T(2,128)(2,1)}, bf16[152,128]{1,0:T(8,128)(2,1)S(1)}) custom-call(bf16[2,34,2,768]{3,2,1,0:T(2,128)(2,1)} %bitcast.12, bf16[136,136]{1,0:T(8,128)(2,1)} %bitcast.13), custom_call_target="tpu_custom_call" | custom-call | tf_op jit(solution)/shard_map/pallas_call | solution.py:220
  3.2 12.9 %all-to-all-start = ((bf16[64,12,2,68]{3,2,1,0:T(2,128)(2,1)}), bf16[64,12,2,68]{3,2,1,0:T(2,128)(2,1)S(1)}, u32[]{:S(2)}, u32[]{:S(2)}) async-start(bf16[64,12,2,68]{3,2,1,0:T(2,128)(2,1)} %bitcast.2), calls=%async_computation | async-start | bytes 786432 | tf_op jit(solution)/shard_map/all_to_all | solution.py:237
  16.2 27.9 %all-gather = bf16[1824,128]{1,0:T(8,128)(2,1)S(1)} all-gather(bf16[152,128]{1,0:T(8,128)(2,1)S(1)} %get-tuple-element.8), channel_id=2, replica_groups=mesh['yh'=2,'zh'=6,'zl'=2,'x'=4,'c'=2,'lev'=4] {'zh','c'}, dimensions={0}, use_global_device_ids=true | all-gather | bytes 505856 | tf_op jit(solution)/shard_map/all_gather | solution.py:238
  44.1 0.0 all-to-all-done
  44.1 0.0 copy-done.1
  44.1 2.4 %shard_map.95 = bf16[16,4,2,1664]{3,2,1,0:T(2,128)(2,1)} custom-call(bf16[16,4,12,2,68]{4,3,2,1,0:T(2,128)(2,1)S(1)} %bitcast.10, bf16[12,152,128]{2,1,0:T(8,128)(2,1)S(1)} %bitcast.9, bf16[136,136]{1,0:T(8,128)(2,1)S(1)} %copy-done.1), custom_call_target="tpu_custom_call" | custom-call | tf_op jit(solution)/shard_map/pallas_call | solution.py:241
  46.5 0.0 copy-start.4
  46.5 0.0 copy-start.2
  46.5 0.0 copy-start.3
  46.6 0.0 copy-start
  46.6 9.9 %all-to-all-start.1 = ((bf16[64,2,1664]{2,1,0:T(2,128)(2,1)}), bf16[64,2,1664]{2,1,0:T(2,128)(2,1)S(1)}, u32[]{:S(2)}, u32[]{:S(2)}) async-start(bf16[64,2,1664]{2,1,0:T(2,128)(2,1)} %bitcast.5), calls=%async_computation.1 | async-start | bytes 851968 | tf_op jit(solution)/shard_map/all_to_all | solution.py:260
  56.5 0.4 shard_map.96.q_ref
  56.9 0.0 copy-done.4
  56.9 0.1 dynamic_slice.3
  57.0 0.0 copy-done.2
  57.0 0.1 iota_compare_fusion
  57.1 0.1 add_divide_fusion
  57.2 0.0 copy-done.3
  57.2 0.9 %broadcast_select_fusion = bf16[2,2,34,768]{3,1,2,0:T(2,128)(2,1)} fusion(pred[2,768]{1,0:T(4,128)(4,1)S(1)} %iota_compare_fusion, bf16[2,2,34,768]{3,1,2,0:T(2,128)(2,1)S(1)} %copy-done.3, f32[34,768]{1,0:T(8,128)S(1)} %add_divide_fusion), kind=kLoop, calls=%fused_computation.1 | loop fusion | flops 417792 | bytes 523776 | tf_op jit(solution)/shard_map/jit(_where)/select_n | solution.py:289
  58.1 14.2 %all-to-all-done.1.b_ref = bf16[64,2,1664]{2,1,0:T(2,128)(2,1)S(1)} async-done(((bf16[64,2,1664]{2,1,0:T(2,128)(2,1)}), bf16[64,2,1664]{2,1,0:T(2,128)(2,1)S(1)}, u32[]{:S(2)}, u32[]{:S(2)}) %all-to-all-start.1) | async-done | bytes 426016 | tf_op jit(solution)/shard_map/all_to_all | solution.py:260
  72.3 0.0 copy-done
  72.3 2.6 %shard_map.97 = (bf16[2,34,2,768]{3,2,1,0:T(2,128)(2,1)}, bf16[2,34,2,768]{3,2,1,0:T(2,128)(2,1)}) custom-call(s32[2]{0:T(128)S(1)} %copy-done.2, bf16[64,2,1664]{2,1,0:T(2,128)(2,1)S(1)} %all-to-all-done.1.b_ref, bf16[2,34,2,768]{3,2,1,0:T(2,128)(2,1)S(1)} %bitcast.11, bf16[768,768]{1,0:T(8,128)(2,1)S(1)} %shard_map.96.q_ref), custom_call_target="tpu_custom_call" | custom-call | tf_op jit(solution)/shard_map/pallas_call | solution.py:266
  (1 shorter events, 0.0 us)
Async XLA Ops:
  0.6 43.5 %copy-start.1 = (bf16[136,136]{1,0:T(8,128)(2,1)S(1)}, bf16[136,136]{1,0:T(8,128)(2,1)}, u32[]{:S(2)}) copy-start(bf16[136,136]{1,0:T(8,128)(2,1)} %c_ref.1) | copy-start | bytes 110980
  3.2 40.8 %all-to-all-start = ((bf16[64,12,2,68]{3,2,1,0:T(2,128)(2,1)}), bf16[64,12,2,68]{3,2,1,0:T(2,128)(2,1)S(1)}, u32[]{:S(2)}, u32[]{:S(2)}) async-start(bf16[64,12,2,68]{3,2,1,0:T(2,128)(2,1)} %bitcast.2), calls=%async_computation | async-start | bytes 786432 | tf_op jit(solution)/shard_map/all_to_all | solution.py:237
  46.5 10.4 %copy-start.4 = (f32[136]{0:T(256)S(1)}, f32[136]{0:T(256)}, u32[]{:S(2)}) copy-start(f32[136]{0:T(256)} %param.12) | copy-start | bytes 1636
  46.5 10.5 %copy-start.2 = (s32[2]{0:T(128)S(1)}, s32[2]{0:T(128)}, u32[]{:S(2)}) copy-start(s32[2]{0:T(128)} %m_ref.1) | copy-start | bytes 28
  46.5 10.6 %copy-start.3 = (bf16[2,2,34,768]{3,1,2,0:T(2,128)(2,1)S(1)}, bf16[2,2,34,768]{3,1,2,0:T(2,128)(2,1)}, u32[]{:S(2)}) copy-start(bf16[2,2,34,768]{3,1,2,0:T(2,128)(2,1)} %param.7) | copy-start | bytes 626692
  46.6 25.8 %copy-start = (bf16[2,2,34,768]{3,1,2,0:T(2,128)(2,1)S(1)}, bf16[2,2,34,768]{3,1,2,0:T(2,128)(2,1)}, u32[]{:S(2)}) copy-start(bf16[2,2,34,768]{3,1,2,0:T(2,128)(2,1)} %param.9) | copy-start | bytes 626692
  46.6 25.7 %all-to-all-start.1 = ((bf16[64,2,1664]{2,1,0:T(2,128)(2,1)}), bf16[64,2,1664]{2,1,0:T(2,128)(2,1)S(1)}, u32[]{:S(2)}, u32[]{:S(2)}) async-start(bf16[64,2,1664]{2,1,0:T(2,128)(2,1)} %bitcast.5), calls=%async_computation.1 | async-start | bytes 851968 | tf_op jit(solution)/shard_map/all_to_all | solution.py:260

commit v8 on v7

--- a/solution.py
+++ b/solution.py
@@ -6,7 +6,7 @@
 from jax.sharding import Mesh, PartitionSpec as P
 
 WAVE = ("yh", "zh", "zl", "x", "c")
-PEERS = ("zl", "x", "yh", "lev")
+PEERS = ("yh", "zl", "lev", "x")
 SHARERS = ("zh", "c")
 NT = (((1,), (1,)), ((), ()))
 NN = (((1,), (0,)), ((), ()))
@@ -61,10 +61,10 @@
             for yh in range(2):
                 for zh in range(6):
                     for zl in range(2):
-                        o_ref[zl, :, yh, 2 * h + l, zh] = both[l, yh, zh, zl]
+                        o_ref[yh, zl, 2 * h + l, :, zh] = both[l, yh, zh, zl]
         part = pl.ds(2 * h, 2)
         leave = pltpu.make_async_copy(
-            o_ref.at[:, :, :, part], o_hbm.at[:, :, :, part], sems.at[2 + h]
+            o_ref.at[:, :, part], o_hbm.at[:, :, part], sems.at[2 + h]
         )
         leave.start()
         leaving.append(leave)
@@ -77,7 +77,7 @@
     for z in range(nz):
         parts = ([], [])
         for l in range(4):
-            pairs[z * 4 + l, :, 0:68] = x_ref[:, l, z].reshape(32, 68).astype(jnp.float32)
+            pairs[z * 4 + l, :, 0:68] = x_ref[:, l, :, z].reshape(32, 68).astype(jnp.float32)
             for c in range(2):
                 parts[c].append(pairs[z * 4 + l, pl.ds(c, 16, 2), :])
         x = jnp.concatenate(
@@ -122,8 +122,8 @@
                         [tile[:, 0:96], jnp.zeros((16, 32), jnp.float32)], axis=1
                     )
                 pairs[l * 13 + t, pl.ds(c, 16, 2), :] = tile
-            o_ref[:, l, :, t * 128 : t * 128 + 128] = (
-                pairs[l * 13 + t].astype(jnp.bfloat16).reshape(16, 2, 128)
+            o_ref[:, l, :, :, t * 128 : t * 128 + 128] = (
+                pairs[l * 13 + t].astype(jnp.bfloat16).reshape(4, 4, 2, 128)
             )
         leave = pltpu.make_async_copy(o_ref.at[:, l], o_hbm.at[:, l], sems.at[l])
         leave.start()
@@ -136,8 +136,8 @@
     for g in range(3):
         row = lax.broadcasted_iota(jnp.int32, (256, 768), 0)
         col = lax.broadcasted_iota(jnp.int32, (256, 768), 1)
-        q, s, l = 4 * g + (row >> 6), (row >> 2) & 15, row & 3
-        zl, x, yh = s >> 3, (s >> 1) & 3, s & 1
+        q, l = 4 * g + (row >> 6), (row >> 2) & 3
+        yh, zl, x = (row >> 5) & 1, (row >> 4) & 1, row & 3
         place = l * 192 + yh * 96 + (q >> 1) * 16 + zl * 8 + x * 2 + (q & 1)
         q_ref[g * 256 : g * 256 + 256, :] = jnp.where(col == place, 1.0, 0.0).astype(
             jnp.bfloat16
@@ -216,7 +216,7 @@
     def room(*shape, dtype=jnp.bfloat16):
         return pltpu.VMEM(shape, dtype)
 
-    outgoing = (nzl, nx, nyh, nlev, nzh, nc, parts, rows * lev_local)
+    outgoing = (nyh, nzl, nlev, nx, nzh, nc, parts, rows * lev_local)
     sent, packed = pl.pallas_call(
         prepare_kernel,
         out_shape=(bf16(*outgoing), bf16(layers + 16, 128)),
@@ -240,19 +240,19 @@
     width = 13 * 128
     both = pl.pallas_call(
         solve_kernel,
-        out_shape=bf16(peers, nlev, parts, width),
+        out_shape=bf16(nyh * nzl, nlev, nx, parts, width),
         in_specs=[VMEM] * 3,
         out_specs=HBM,
         scratch_shapes=[
             room(nlev, parts, peers, width, dtype=jnp.float32),
             room(shared * parts * rows * peers, layers),
-            room(peers, nlev, parts, width),
+            room(nyh * nzl, nlev, nx, parts, width),
             room(nlev * 13, parts * peers, 128, dtype=jnp.float32),
             copies(4),
         ],
         compiler_params=LIMIT,
     )(
-        got.reshape(peers, nlev, shared, parts, rows * lev_local),
+        got.reshape(nyh * nzl, nlev, nx, shared, parts, rows * lev_local),
         matrices,
         heat_spreading_coupler,
     )

time: 75.2 us -> 74.9 us (level)
  waiting for transfers between devices: 14.2 us -> 13.1 us
    all_to_all x1, waiting for transfers between devices: 14.2 us -> 13.1 us  [on_device(): back = lax.all_to_all(both, PEERS, split_axis=0, concat_axis=0, tiled=True)]
where the time goes in v8:
time: 74.9 us; the launch traced here: 73.9 us
  blocking collectives  27.9 us (37%)
  starting transfers between devices  22.9 us (31%)
  waiting for transfers between devices  13.1 us (17%)
  Pallas kernels  8.05 us (11%)
  other arithmetic  1.08 us (1%)
    all_gather x1, blocking collectives, on_device(): matrices = lax.all_gather(packed, SHARERS, axis=0, tiled=False)  27.9 us
    all_to_all x1, waiting for transfers between devices, on_device(): back = lax.all_to_all(both, PEERS, split_axis=0, concat_axis=0, tiled=True)  13.1 us
    all_to_all x1, starting transfers between devices, on_device(): got = lax.all_to_all(sent, PEERS, split_axis=0, concat_axis=0, tiled=True)  12.9 us
    all_to_all x1, starting transfers between devices, on_device(): back = lax.all_to_all(both, PEERS, split_axis=0, concat_axis=0, tiled=True)  9.96 us
    pallas_call x1, Pallas kernels, on_device(): pl.pallas_call(finish_kernel, out_shape=(bf16(*spectrum), bf16(*spectrum)...  2.64 us
    pallas_call x1, Pallas kernels, on_device(): pl.pallas_call(prepare_kernel, out_shape=(bf16(*outgoing), bf16(layers +...  2.58 us
    pallas_call x1, Pallas kernels, on_device(): pl.pallas_call(solve_kernel, out_shape=bf16(nyh * nzl, nlev, nx, parts, w...  2.41 us
  transfers between devices with their start and end apart: 2, of which 1 were waited for; matrix products, arithmetic and copies ran while one was open for 2% of the time, Pallas kernels for 1%

profile of v8, /device:TPU:1, one launch (start us, length us, event | category | flops | bytes accessed | tf_op | source)
XLA Modules:
  0.0 73.9 jit_solution(7784857947630189081)
XLA Ops:
  0.6 0.0 copy-start.1
  0.6 2.6 %shard_map.94 = (bf16[2,2,4,4,6,2,2,68]{7,6,5,4,3,2,1,0:T(2,128)(2,1)}, bf16[152,128]{1,0:T(8,128)(2,1)S(1)}) custom-call(bf16[2,34,2,768]{3,2,1,0:T(2,128)(2,1)} %bitcast.12, bf16[136,136]{1,0:T(8,128)(2,1)} %bitcast.13), custom_call_target="tpu_custom_call" | custom-call | tf_op jit(solution)/shard_map/pallas_call | solution.py:220
  3.2 12.9 %all-to-all-start = ((bf16[64,12,2,68]{3,2,1,0:T(2,128)(2,1)}), bf16[64,12,2,68]{3,2,1,0:T(2,128)(2,1)S(1)}, u32[]{:S(2)}, u32[]{:S(2)}) async-start(bf16[64,12,2,68]{3,2,1,0:T(2,128)(2,1)} %bitcast.2), calls=%async_computation | async-start | bytes 786432 | tf_op jit(solution)/shard_map/all_to_all | solution.py:237
  16.2 27.9 %all-gather = bf16[1824,128]{1,0:T(8,128)(2,1)S(1)} all-gather(bf16[152,128]{1,0:T(8,128)(2,1)S(1)} %get-tuple-element.8), channel_id=2, replica_groups=mesh['yh'=2,'zh'=6,'zl'=2,'x'=4,'c'=2,'lev'=4] {'zh','c'}, dimensions={0}, use_global_device_ids=true | all-gather | bytes 505856 | tf_op jit(solution)/shard_map/all_gather | solution.py:238
  44.1 0.0 all-to-all-done
  44.1 0.0 copy-done.1
  44.1 2.4 %shard_map.95 = bf16[4,4,4,2,1664]{4,3,2,1,0:T(2,128)(2,1)} custom-call(bf16[4,4,4,12,2,68]{5,4,3,2,1,0:T(2,128)(2,1)S(1)} %bitcast.10, bf16[12,152,128]{2,1,0:T(8,128)(2,1)S(1)} %bitcast.9, bf16[136,136]{1,0:T(8,128)(2,1)S(1)} %copy-done.1), custom_call_target="tpu_custom_call" | custom-call | tf_op jit(solution)/shard_map/pallas_call | solution.py:241
  46.5 0.0 copy-start.4
  46.5 0.0 copy-start.2
  46.5 0.0 copy-start.3
  46.6 0.0 copy-start
  46.6 10.0 %all-to-all-start.1 = ((bf16[64,2,1664]{2,1,0:T(2,128)(2,1)}), bf16[64,2,1664]{2,1,0:T(2,128)(2,1)S(1)}, u32[]{:S(2)}, u32[]{:S(2)}) async-start(bf16[64,2,1664]{2,1,0:T(2,128)(2,1)} %bitcast.5), calls=%async_computation.1 | async-start | bytes 851968 | tf_op jit(solution)/shard_map/all_to_all | solution.py:260
  56.5 0.4 shard_map.96.q_ref
  57.0 0.0 copy-done.4
  57.0 0.1 dynamic_slice.3
  57.1 0.0 copy-done.2
  57.1 0.1 iota_compare_fusion
  57.1 0.1 add_divide_fusion
  57.2 0.0 copy-done.3
  57.3 0.9 %broadcast_select_fusion = bf16[2,2,34,768]{3,1,2,0:T(2,128)(2,1)} fusion(pred[2,768]{1,0:T(4,128)(4,1)S(1)} %iota_compare_fusion, bf16[2,2,34,768]{3,1,2,0:T(2,128)(2,1)S(1)} %copy-done.3, f32[34,768]{1,0:T(8,128)S(1)} %add_divide_fusion), kind=kLoop, calls=%fused_computation.1 | loop fusion | flops 417792 | bytes 523776 | tf_op jit(solution)/shard_map/jit(_where)/select_n | solution.py:289
  58.2 13.1 %all-to-all-done.1.b_ref = bf16[64,2,1664]{2,1,0:T(2,128)(2,1)S(1)} async-done(((bf16[64,2,1664]{2,1,0:T(2,128)(2,1)}), bf16[64,2,1664]{2,1,0:T(2,128)(2,1)S(1)}, u32[]{:S(2)}, u32[]{:S(2)}) %all-to-all-start.1) | async-done | bytes 426016 | tf_op jit(solution)/shard_map/all_to_all | solution.py:260
  71.3 0.0 copy-done
  71.3 2.6 %shard_map.97 = (bf16[2,34,2,768]{3,2,1,0:T(2,128)(2,1)}, bf16[2,34,2,768]{3,2,1,0:T(2,128)(2,1)}) custom-call(s32[2]{0:T(128)S(1)} %copy-done.2, bf16[64,2,1664]{2,1,0:T(2,128)(2,1)S(1)} %all-to-all-done.1.b_ref, bf16[2,34,2,768]{3,2,1,0:T(2,128)(2,1)S(1)} %bitcast.11, bf16[768,768]{1,0:T(8,128)(2,1)S(1)} %shard_map.96.q_ref), custom_call_target="tpu_custom_call" | custom-call | tf_op jit(solution)/shard_map/pallas_call | solution.py:266
  (1 shorter events, 0.0 us)
Async XLA Ops:
  0.6 43.5 %copy-start.1 = (bf16[136,136]{1,0:T(8,128)(2,1)S(1)}, bf16[136,136]{1,0:T(8,128)(2,1)}, u32[]{:S(2)}) copy-start(bf16[136,136]{1,0:T(8,128)(2,1)} %c_ref.1) | copy-start | bytes 110980
  3.2 40.9 %all-to-all-start = ((bf16[64,12,2,68]{3,2,1,0:T(2,128)(2,1)}), bf16[64,12,2,68]{3,2,1,0:T(2,128)(2,1)S(1)}, u32[]{:S(2)}, u32[]{:S(2)}) async-start(bf16[64,12,2,68]{3,2,1,0:T(2,128)(2,1)} %bitcast.2), calls=%async_computation | async-start | bytes 786432 | tf_op jit(solution)/shard_map/all_to_all | solution.py:237
  46.5 10.5 %copy-start.4 = (f32[136]{0:T(256)S(1)}, f32[136]{0:T(256)}, u32[]{:S(2)}) copy-start(f32[136]{0:T(256)} %param.12) | copy-start | bytes 1636
  46.5 10.5 %copy-start.2 = (s32[2]{0:T(128)S(1)}, s32[2]{0:T(128)}, u32[]{:S(2)}) copy-start(s32[2]{0:T(128)} %m_ref.1) | copy-start | bytes 28
  46.5 10.7 %copy-start.3 = (bf16[2,2,34,768]{3,1,2,0:T(2,128)(2,1)S(1)}, bf16[2,2,34,768]{3,1,2,0:T(2,128)(2,1)}, u32[]{:S(2)}) copy-start(bf16[2,2,34,768]{3,1,2,0:T(2,128)(2,1)} %param.7) | copy-start | bytes 626692
  46.6 24.7 %copy-start = (bf16[2,2,34,768]{3,1,2,0:T(2,128)(2,1)S(1)}, bf16[2,2,34,768]{3,1,2,0:T(2,128)(2,1)}, u32[]{:S(2)}) copy-start(bf16[2,2,34,768]{3,1,2,0:T(2,128)(2,1)} %param.9) | copy-start | bytes 626692
  46.6 24.7 %all-to-all-start.1 = ((bf16[64,2,1664]{2,1,0:T(2,128)(2,1)}), bf16[64,2,1664]{2,1,0:T(2,128)(2,1)S(1)}, u32[]{:S(2)}, u32[]{:S(2)}) async-start(bf16[64,2,1664]{2,1,0:T(2,128)(2,1)} %bitcast.5), calls=%async_computation.1 | async-start | bytes 851968 | tf_op jit(solution)/shard_map/all_to_all | solution.py:260

commit v9 on v5

--- a/solution.py
+++ b/solution.py
@@ -39,7 +39,7 @@
     ).astype(jnp.bfloat16)
 
 
-def prepare_kernel(x_hbm, m_hbm, o_hbm, p_ref, x_ref, m_ref, o_ref, sems):
+def prepare_kernel(x_hbm, m_hbm, o_hbm, p_ref, x_ref, m_ref, o_ref, pairs, sems):
     load_m = pltpu.make_async_copy(m_hbm, m_ref, sems.at[0])
     load_m.start()
     load_x = pltpu.make_async_copy(x_hbm, x_ref, sems.at[1])
@@ -49,14 +49,13 @@
     load_x.wait()
     leaving = []
     for h in range(2):
-        sides = []
         for c in range(2):
             x = x_ref[:, :, :, h * 384 : h * 384 + 384].astype(jnp.float32)
             rows = jnp.concatenate(
                 [x[0, :, c, :], x[1, :, c, :], jnp.zeros((4, 384), jnp.float32)], axis=0
             )
-            sides.append(rows.T[:, 0:68])
-        both = jnp.stack(sides, axis=1).astype(jnp.bfloat16).reshape(2, 2, 6, 2, 4, 2, 2, 68)
+            pairs[h, pl.ds(c, 384, 2), 0:68] = rows.T[:, 0:68]
+        both = pairs[h, :, 0:68].astype(jnp.bfloat16).reshape(2, 2, 6, 2, 4, 2, 2, 68)
         for l in range(2):
             for yh in range(2):
                 for zh in range(6):
@@ -226,6 +225,7 @@
             room(rows, lev_local, parts, total_n),
             room(layers, layers),
             room(*outgoing),
+            room(2, parts * total_n // 2, 128, dtype=jnp.float32),
             copies(4),
         ],
         compiler_params=LIMIT,

time: 73.7 us -> 73.3 us (level)
  no operation moved by 1% of the time
where the time goes in v9:
time: 73.3 us; the launch traced here: 72.7 us
  blocking collectives  27.8 us (38%)
  starting transfers between devices  23 us (31%)
  waiting for transfers between devices  12.2 us (17%)
  Pallas kernels  7.69 us (10%)
  other arithmetic  1.08 us (1%)
  between operations  0.74 us (1%)
    all_gather x1, blocking collectives, on_device(): matrices = lax.all_gather(packed, SHARERS, axis=0, tiled=False)  27.8 us
    all_to_all x1, starting transfers between devices, on_device(): got = lax.all_to_all(sent, PEERS, split_axis=0, concat_axis=0, tiled=True)  12.9 us
    all_to_all x1, waiting for transfers between devices, on_device(): back = lax.all_to_all(both, PEERS, split_axis=0, concat_axis=0, tiled=True)  12.2 us
    all_to_all x1, starting transfers between devices, on_device(): back = lax.all_to_all(both, PEERS, split_axis=0, concat_axis=0, tiled=True)  10.1 us
    pallas_call x1, Pallas kernels, on_device(): pl.pallas_call(finish_kernel, out_shape=(bf16(*spectrum), bf16(*spectrum)...  2.64 us
    pallas_call x1, Pallas kernels, on_device(): pl.pallas_call(solve_kernel, out_shape=bf16(peers, nlev, parts, width), i...  2.42 us
    pallas_call x1, Pallas kernels, on_device(): pl.pallas_call(prepare_kernel, out_shape=(bf16(*outgoing), bf16(layers +...  2.22 us
  transfers between devices with their start and end apart: 2, of which 1 were waited for; matrix products, arithmetic and copies ran while one was open for 2% of the time, Pallas kernels for 1%

profile of v9, /device:TPU:1, one launch (start us, length us, event | category | flops | bytes accessed | tf_op | source)
XLA Modules:
  0.0 72.7 jit_solution(10676843135995591523)
XLA Ops:
  0.6 0.0 copy-start.1
  0.6 2.2 %shard_map.94 = (bf16[2,2,4,4,6,2,2,68]{7,6,5,4,3,2,1,0:T(2,128)(2,1)}, bf16[152,128]{1,0:T(8,128)(2,1)S(1)}) custom-call(bf16[2,34,2,768]{3,2,1,0:T(2,128)(2,1)} %bitcast.12, bf16[136,136]{1,0:T(8,128)(2,1)} %bitcast.13), custom_call_target="tpu_custom_call" | custom-call | tf_op jit(solution)/shard_map/pallas_call | solution.py:219
  2.9 12.9 %all-to-all-start = ((bf16[64,12,2,68]{3,2,1,0:T(2,128)(2,1)}), bf16[64,12,2,68]{3,2,1,0:T(2,128)(2,1)S(1)}, u32[]{:S(2)}, u32[]{:S(2)}) async-start(bf16[64,12,2,68]{3,2,1,0:T(2,128)(2,1)} %bitcast.2), calls=%async_computation | async-start | bytes 786432 | tf_op jit(solution)/shard_map/all_to_all | solution.py:237
  15.8 27.8 %all-gather = bf16[1824,128]{1,0:T(8,128)(2,1)S(1)} all-gather(bf16[152,128]{1,0:T(8,128)(2,1)S(1)} %get-tuple-element.8), channel_id=2, replica_groups=mesh['yh'=2,'zh'=6,'zl'=2,'x'=4,'c'=2,'lev'=4] {'zh','c'}, dimensions={0}, use_global_device_ids=true | all-gather | bytes 505856 | tf_op jit(solution)/shard_map/all_gather | solution.py:238
  43.6 0.0 all-to-all-done
  43.6 0.0 copy-done.1
  43.6 2.4 %shard_map.95 = bf16[16,4,2,1664]{3,2,1,0:T(2,128)(2,1)} custom-call(bf16[16,4,12,2,68]{4,3,2,1,0:T(2,128)(2,1)S(1)} %bitcast.10, bf16[12,152,128]{2,1,0:T(8,128)(2,1)S(1)} %bitcast.9, bf16[136,136]{1,0:T(8,128)(2,1)S(1)} %copy-done.1), custom_call_target="tpu_custom_call" | custom-call | tf_op jit(solution)/shard_map/pallas_call | solution.py:241
  46.1 0.0 copy-start.4
  46.1 0.0 copy-start.2
  46.1 0.0 copy-start.3
  46.1 0.0 copy-start
  46.1 10.1 %all-to-all-start.1 = ((bf16[64,2,1664]{2,1,0:T(2,128)(2,1)}), bf16[64,2,1664]{2,1,0:T(2,128)(2,1)S(1)}, u32[]{:S(2)}, u32[]{:S(2)}) async-start(bf16[64,2,1664]{2,1,0:T(2,128)(2,1)} %bitcast.5), calls=%async_computation.1 | async-start | bytes 851968 | tf_op jit(solution)/shard_map/all_to_all | solution.py:260
  56.2 0.4 shard_map.96.q_ref
  56.7 0.0 copy-done.4
  56.7 0.1 dynamic_slice.3
  56.8 0.0 copy-done.2
  56.8 0.1 iota_compare_fusion
  56.8 0.1 add_divide_fusion
  56.9 0.0 copy-done.3
  56.9 0.9 %broadcast_select_fusion = bf16[2,2,34,768]{3,1,2,0:T(2,128)(2,1)} fusion(pred[2,768]{1,0:T(4,128)(4,1)S(1)} %iota_compare_fusion, bf16[2,2,34,768]{3,1,2,0:T(2,128)(2,1)S(1)} %copy-done.3, f32[34,768]{1,0:T(8,128)S(1)} %add_divide_fusion), kind=kLoop, calls=%fused_computation.1 | loop fusion | flops 417792 | bytes 523776 | tf_op jit(solution)/shard_map/jit(_where)/select_n | solution.py:289
  57.8 12.2 %all-to-all-done.1.b_ref = bf16[64,2,1664]{2,1,0:T(2,128)(2,1)S(1)} async-done(((bf16[64,2,1664]{2,1,0:T(2,128)(2,1)}), bf16[64,2,1664]{2,1,0:T(2,128)(2,1)S(1)}, u32[]{:S(2)}, u32[]{:S(2)}) %all-to-all-start.1) | async-done | bytes 426016 | tf_op jit(solution)/shard_map/all_to_all | solution.py:260
  70.0 0.0 copy-done
  70.0 2.6 %shard_map.97 = (bf16[2,34,2,768]{3,2,1,0:T(2,128)(2,1)}, bf16[2,34,2,768]{3,2,1,0:T(2,128)(2,1)}) custom-call(s32[2]{0:T(128)S(1)} %copy-done.2, bf16[64,2,1664]{2,1,0:T(2,128)(2,1)S(1)} %all-to-all-done.1.b_ref, bf16[2,34,2,768]{3,2,1,0:T(2,128)(2,1)S(1)} %bitcast.11, bf16[768,768]{1,0:T(8,128)(2,1)S(1)} %shard_map.96.q_ref), custom_call_target="tpu_custom_call" | custom-call | tf_op jit(solution)/shard_map/pallas_call | solution.py:266
  (1 shorter events, 0.0 us)
Async XLA Ops:
  0.6 43.0 %copy-start.1 = (bf16[136,136]{1,0:T(8,128)(2,1)S(1)}, bf16[136,136]{1,0:T(8,128)(2,1)}, u32[]{:S(2)}) copy-start(bf16[136,136]{1,0:T(8,128)(2,1)} %c_ref.1) | copy-start | bytes 110980
  2.9 40.8 %all-to-all-start = ((bf16[64,12,2,68]{3,2,1,0:T(2,128)(2,1)}), bf16[64,12,2,68]{3,2,1,0:T(2,128)(2,1)S(1)}, u32[]{:S(2)}, u32[]{:S(2)}) async-start(bf16[64,12,2,68]{3,2,1,0:T(2,128)(2,1)} %bitcast.2), calls=%async_computation | async-start | bytes 786432 | tf_op jit(solution)/shard_map/all_to_all | solution.py:237
  46.1 10.6 %copy-start.4 = (f32[136]{0:T(256)S(1)}, f32[136]{0:T(256)}, u32[]{:S(2)}) copy-start(f32[136]{0:T(256)} %param.12) | copy-start | bytes 1636
  46.1 10.7 %copy-start.2 = (s32[2]{0:T(128)S(1)}, s32[2]{0:T(128)}, u32[]{:S(2)}) copy-start(s32[2]{0:T(128)} %m_ref.1) | copy-start | bytes 28
  46.1 10.8 %copy-start.3 = (bf16[2,2,34,768]{3,1,2,0:T(2,128)(2,1)S(1)}, bf16[2,2,34,768]{3,1,2,0:T(2,128)(2,1)}, u32[]{:S(2)}) copy-start(bf16[2,2,34,768]{3,1,2,0:T(2,128)(2,1)} %param.7) | copy-start | bytes 626692
  46.1 23.9 %copy-start = (bf16[2,2,34,768]{3,1,2,0:T(2,128)(2,1)S(1)}, bf16[2,2,34,768]{3,1,2,0:T(2,128)(2,1)}, u32[]{:S(2)}) copy-start(bf16[2,2,34,768]{3,1,2,0:T(2,128)(2,1)} %param.9) | copy-start | bytes 626692
  46.1 23.9 %all-to-all-start.1 = ((bf16[64,2,1664]{2,1,0:T(2,128)(2,1)}), bf16[64,2,1664]{2,1,0:T(2,128)(2,1)S(1)}, u32[]{:S(2)}, u32[]{:S(2)}) async-start(bf16[64,2,1664]{2,1,0:T(2,128)(2,1)} %bitcast.5), calls=%async_computation.1 | async-start | bytes 851968 | tf_op jit(solution)/shard_map/all_to_all | solution.py:260
